TPU v7x, 256 devices: a whole 4x4x8 slice. The times are simulated.
256 devices in a mesh: seq: 64 (over z, y, core), head: 4 (over x).
Axes of the slice: x: 4, y: 4, z: 8, core: 2. Of those that a mesh axis runs over, the one named last changes fastest.
Arguments:
- query_rows: bfloat16 [131072, 4096], P(('seq', 'head')), may hold values from -200 to 200
- key_rows: bfloat16 [131072, 512], P(('seq', 'head')), may hold values from -18 to 18
- value_rows: bfloat16 [131072, 512], P(('seq', 'head')), may hold values from -6 to 6
- random_table: int32 [1024, 4, 3], replicated, may hold values from 0 to 1023, as said below
- global_blocks: int32 [2], replicated, may hold values from 0 to 1023
Outputs:
- attended: bfloat16 [131072, 4096], P(('seq', 'head'))
Inputs may be any that keep to these rules, and one draw needn't show every extreme that they name: `random_table`: for each of the 4 head groups and each aligned run of 16 query blocks (those of one index of seq), with the owner of block j being j // 16: at most 2 of the run's 3 * 16 entries name blocks of one owner, and they name at most 1 distinct blocks of one owner; both bounds are reached.
All inputs are finite; a program needn't handle non-finite values.
Results may differ from a plain program's by a relative error of at most 0.0029.
Values may be sent and summed in bfloat16 or wider, within the bound.
A program may use at most 128 MiB of HBM per device.

v0:
```python
import math

import jax
import jax.numpy as jnp
from jax import lax
from jax.sharding import PartitionSpec as P

BLOCK = 128
HEAD_DIM = 128
GLOBALS = 2
RANDOM = 3


def padded_2(cells, sides, width):
    for axis, dim in sides:
        count = lax.axis_size(axis)
        ends = count - 1
        head = lax.slice_in_dim(cells, 0, width, axis=dim)
        tail = lax.slice_in_dim(cells, cells.shape[dim] - width, cells.shape[dim], axis=dim)
        cells = jnp.concatenate(
            [
                lax.ppermute(tail, axis, [(i, (i + 1) % count) for i in range(ends)]),
                cells,
                lax.ppermute(head, axis, [((i + 1) % count, i) for i in range(ends)]),
            ],
            axis=dim,
        )
    return cells


def picked(shard, axis, root):
    return lax.dynamic_index_in_dim(lax.all_gather(shard, axis), root, 0, keepdims=False)


def attend_group(query_group, context, usable, score_scale):
    key_part = context[..., :HEAD_DIM]
    values = context[..., HEAD_DIM:]
    scores = (
        jnp.einsum("ptgd,psd->pgts", query_group, key_part, preferred_element_type=jnp.float32)
        * score_scale
    )
    scores = jnp.where(usable[:, None, None, :], scores, -1e30)
    row_max = jnp.max(scores, axis=-1, keepdims=True)
    weights = jnp.exp(scores - row_max)
    row_total = jnp.sum(weights, axis=-1)
    rounded = weights.astype(jnp.bfloat16)
    mixed = jnp.einsum("pgts,psd->ptgd", rounded, values, preferred_element_type=jnp.float32)
    mixed = mixed / jnp.transpose(row_total, (0, 2, 1))[..., None]
    return mixed.astype(jnp.bfloat16)


def on_device(query_rows, key_rows, value_rows, random_table, global_blocks):
    queries, key_part, values = (
        lax.all_to_all(query_rows, "head", split_axis=1, concat_axis=0, tiled=True),
        lax.all_to_all(key_rows, "head", split_axis=1, concat_axis=0, tiled=True),
        lax.all_to_all(value_rows, "head", split_axis=1, concat_axis=0, tiled=True),
    )
    local_rows = queries.shape[0]
    block_count = local_rows // BLOCK
    grouping = queries.shape[1] // HEAD_DIM
    seq_count = lax.axis_size("seq")
    seq_index = lax.axis_index("seq")
    head_index = lax.axis_index("head")
    paired = jnp.concatenate([key_part, values], axis=1)
    local_blocks = paired.reshape(block_count, BLOCK, 2 * HEAD_DIM)
    padded = padded_2(paired, (("seq", 0),), BLOCK)
    global_parts = []
    for global_index in range(GLOBALS):
        named_block = global_blocks[global_index]
        piece = lax.dynamic_index_in_dim(local_blocks, named_block % block_count, 0, keepdims=False)
        global_parts.append(picked(piece, "seq", named_block // block_count))
    shared = jnp.stack(global_parts)
    table_head = lax.dynamic_index_in_dim(random_table, head_index, 1, keepdims=False)
    all_refs = table_head.reshape(seq_count, block_count * RANDOM)
    my_refs = lax.dynamic_index_in_dim(all_refs, seq_index, 0, keepdims=False)
    owner_all = all_refs // block_count
    local_all = all_refs % block_count
    my_owner = my_refs // block_count
    my_local = my_refs % block_count
    entry_bound = 2 * max(1, (RANDOM * block_count + 2 * seq_count - 1) // (2 * seq_count))
    capacity = entry_bound // 2
    block_range = jnp.arange(block_count, dtype=jnp.int32)
    hits = (owner_all[:, :, None] == seq_index) & (local_all[:, :, None] == block_range)
    requested = jnp.any(hits, axis=1)
    distinct_rank = jnp.cumsum(requested.astype(jnp.int32), axis=1) - 1
    selected = requested[:, :, None] & (
        distinct_rank[:, :, None] == jnp.arange(capacity, dtype=jnp.int32)
    )
    sources = jnp.sum(jnp.where(selected, block_range[None, :, None], 0), axis=1)
    filled = jnp.any(selected, axis=1)
    outgoing = jnp.take(local_blocks, sources, axis=0)
    outgoing = jnp.where(filled[:, :, None, None], outgoing, jnp.zeros_like(outgoing))
    received = lax.all_to_all(outgoing, "seq", split_axis=0, concat_axis=0, tiled=True)
    my_requested = jnp.any(
        my_refs[:, None] == jnp.arange(seq_count * block_count, dtype=jnp.int32)[None, :], axis=0
    )
    owner_lines = my_requested.reshape(seq_count, block_count)[my_owner]
    my_slot = jnp.sum(
        (owner_lines & (block_range[None, :] < my_local[:, None])).astype(jnp.int32), axis=1
    )
    fetched = received[my_owner, my_slot].reshape(block_count, RANDOM * BLOCK, 2 * HEAD_DIM)
    previous = padded[:local_rows].reshape(block_count, BLOCK, 2 * HEAD_DIM)
    upcoming = padded[2 * BLOCK :].reshape(block_count, BLOCK, 2 * HEAD_DIM)
    shared_all = jnp.broadcast_to(
        shared.reshape(1, GLOBALS * BLOCK, 2 * HEAD_DIM),
        (block_count, GLOBALS * BLOCK, 2 * HEAD_DIM),
    )
    context = jnp.concatenate([previous, local_blocks, upcoming, shared_all, fetched], axis=1)
    global_ids = seq_index * block_count + jnp.arange(block_count, dtype=jnp.int32)
    block_flags = jnp.concatenate(
        [
            (global_ids > 0)[:, None],
            (global_ids >= 0)[:, None],
            (global_ids < seq_count * block_count - 1)[:, None],
            jnp.ones((block_count, GLOBALS + RANDOM), dtype=bool),
        ],
        axis=1,
    )
    usable = jnp.repeat(block_flags, BLOCK, axis=1)
    per_step = max((size_try for size_try in (1, 2, 3, 4) if block_count % size_try == 0))
    step_count = block_count // per_step
    score_scale = 1.0 / math.sqrt(HEAD_DIM)
    query_steps = queries.reshape(step_count, per_step, BLOCK, grouping, HEAD_DIM)
    context_steps = context.reshape(step_count, per_step, context.shape[1], 2 * HEAD_DIM)
    usable_steps = usable.reshape(step_count, per_step, usable.shape[1])

    def one_step(inputs):
        return attend_group(inputs[0], inputs[1], inputs[2], score_scale)

    mixed = lax.map(one_step, (query_steps, context_steps, usable_steps))
    output_rows = mixed.reshape(local_rows, grouping * HEAD_DIM)
    return lax.all_to_all(output_rows, "head", split_axis=0, concat_axis=1, tiled=True)


def solution(mesh):
    placed = (
        P(("seq", "head"), None),
        P(("seq", "head"), None),
        P(("seq", "head"), None),
        P(),
        P(),
    )
    return jax.shard_map(
        on_device, mesh=mesh, in_specs=placed, out_specs=P(("seq", "head"), None), check_vma=False
    )
```

profile of v0, /device:TPU:1, one launch (start us, length us, event | category | flops | bytes accessed | tf_op | source)
XLA Modules:
  0.0 373.1 jit_solution(15213330352972939691)
XLA Ops:
  6.5 1.0 copy-done
  7.6 0.9 copy_bitcast_fusion.4
  8.5 4.8 %all-to-all-start = ((bf16[512,4,128]{2,0,1:T(8,128)(2,1)}), bf16[512,4,128]{2,0,1:T(8,128)(2,1)S(1)}, u32[]{:S(2)}, u32[]{:S(2)}) async-start(bf16[512,4,128]{2,0,1:T(8,128)(2,1)} %copy_bitcast_fusion.4), calls=%async_computation | async-start | bytes 1048576 | tf_op jit(solution)/shard_map/all_to_all | solution.py:55
  13.3 1.9 copy_bitcast_fusion.3
  15.2 5.5 %all-to-all-done = bf16[512,4,128]{2,0,1:T(8,128)(2,1)S(1)} async-done(((bf16[512,4,128]{2,0,1:T(8,128)(2,1)}), bf16[512,4,128]{2,0,1:T(8,128)(2,1)S(1)}, u32[]{:S(2)}, u32[]{:S(2)}) %all-to-all-start) | async-done | bytes 524320 | tf_op jit(solution)/shard_map/all_to_all | solution.py:55
  20.8 3.5 all-to-all-start.1
  24.3 0.6 fusion.40
  28.8 2.3 all-to-all-done.1
  31.1 0.7 fusion.20
  31.8 4.7 %copy.90 = bf16[64,4,8,1024]{3,2,0,1:T(8,128)(2,1)} copy(bf16[64,4,8,1024]{3,2,1,0:T(8,128)(2,1)} %bitcast.165) | data formatting | bytes 8388608 | tf_op jit(solution)/shard_map/all_to_all | solution.py:54
  36.6 4.9 %all-to-all-start.3 = ((bf16[512,4,1024]{2,0,1:T(8,128)(2,1)}), bf16[512,4,1024]{2,0,1:T(8,128)(2,1)}, u32[]{:S(2)}, u32[]{:S(2)}) async-start(bf16[512,4,1024]{2,0,1:T(8,128)(2,1)} %bitcast.159), calls=%async_computation.3 | async-start | bytes 8388608 | tf_op jit(solution)/shard_map/all_to_all | solution.py:54
  41.5 0.8 constant_dynamic-slice_fusion.2
  43.9 2.8 gather_fusion
  46.7 4.0 %fusion.16 = bf16[64,1,128,256]{3,2,1,0:T(8,128)(2,1)} fusion(bf16[64,128,256]{2,1,0:T(8,128)(2,1)} %gather_fusion, pred[64]{0:T(512)(128)(4,1)S(1)} %compare_and_fusion, pred[64]{0:T(512)(128)(4,1)S(1)} %get-tuple-element.70), kind=kLoop, calls=%fused_computation.27 | loop fusion | flops 4194304 | bytes 8388736 | tf_op jit(solution)/shard_map/jit(_where)/select_n | solution.py:92
  50.7 35.6 %all-to-all-done.3 = bf16[512,4,1024]{2,0,1:T(8,128)(2,1)} async-done(((bf16[512,4,1024]{2,0,1:T(8,128)(2,1)}), bf16[512,4,1024]{2,0,1:T(8,128)(2,1)}, u32[]{:S(2)}, u32[]{:S(2)}) %all-to-all-start.3) | async-done | bytes 4194336 | tf_op jit(solution)/shard_map/all_to_all | solution.py:54
  86.3 17.9 %all-to-all-start.2 = ((bf16[64,1,128,256]{3,2,1,0:T(8,128)(2,1)}), bf16[64,1,128,256]{3,2,1,0:T(8,128)(2,1)}, u32[]{:S(2)}, u32[]{:S(2)}) async-start(bf16[64,1,128,256]{3,2,1,0:T(8,128)(2,1)} %fusion.16), calls=%async_computation.2 | async-start | bytes 8388608 | tf_op jit(solution)/shard_map/all_to_all | solution.py:93
  104.5 0.6 gather_fusion.1
  105.5 3.5 collective-permute-start
  109.0 1.9 collective-permute-start.1
  112.5 2.1 collective-permute-done
  114.5 2.6 collective-permute-done.1
  117.3 1.1 constant_dynamic-update-slice_fusion.3
  118.4 1.1 maximum_dynamic-update-slice_fusion
  119.5 1.1 constant_dynamic-update-slice_fusion.2
  120.6 5.2 %copy.82 = bf16[256,8,8,128]{3,2,1,0:T(8,128)(2,1)} copy(bf16[256,8,8,128]{3,1,2,0:T(8,128)(2,1)} %bitcast.53) | data formatting | bytes 8388608
  125.8 0.8 constant_dynamic-slice_fusion.3
  126.6 88.3 %all-gather.3.cloned.1.call-done = bf16[64,128,256]{2,1,0:T(8,128)(2,1)} async-done(((bf16[1,128,256]{2,1,0:T(8,128)(2,1)}), bf16[64,128,256]{2,1,0:T(8,128)(2,1)}) %all-gather.3.cloned.1.call-update) | async-done | bytes 4194320 | tf_op jit(solution)/shard_map/all_gather | solution.py:32
  215.0 0.8 constant_dynamic-slice_fusion.4
  215.8 1.5 broadcast_dynamic-update-slice_fusion
  217.4 4.6 %gather_fusion.2 = bf16[48,128,256]{2,1,0:T(8,128)(2,1)} fusion(bf16[64,1,128,256]{3,2,1,0:T(8,128)(2,1)} %all-to-all-done.2, s32[48]{0:T(128)S(1)} %fusion.35), kind=kCustom, calls=%fused_computation.2 | custom fusion | bytes 6291840 | tf_op jit(solution)/shard_map/gather | solution.py:101
  222.0 3.8 %constant_dynamic-update-slice_fusion.1 = bf16[4,4,1024,256]{3,2,1,0:T(8,128)(2,1)} fusion(bf16[4,4,1024,256]{3,2,1,0:T(8,128)(2,1)} %broadcast_dynamic-update-slice_fusion, bf16[4,4,384,256]{3,2,1,0:T(8,128)(2,1)} %bitcast.162), kind=kLoop, calls=%fused_computation.66 | loop fusion | bytes 6291456 | tf_op jit(solution)/shard_map/concatenate | solution.py:108
  225.8 66.2 %while.10 = (s32[]{:T(128)}, bf16[4,4,128,8,128]{4,3,2,1,0:T(8,128)(2,1)}, bf16[4,4,1024,256]{3,2,1,0:T(8,128)(2,1)}, pred[4,4,1024]{2,1,0:T(4,128)(4,1)S(1)}, bf16[4,4,128,8,128]{4,3,2,1,0:T(8,128)(2,1)}, /*index=5*/s32[]{:T(128)}) while((s32[]{:T(128)}, bf16[4,4,128,8,128]{4,3,2,1,0:T(8,128)(2,1)}, bf16[4,4,1024,256]{3,2,1,0:T(8,128)(2,1)}, ...), condition=%wide.region_9.10_spmd, body=%wide.region_6.9_spmd.sunk | while | flops 2194661376 | bytes 65114704 | solution.py:130
  225.8 1.7 dynamic-slice_bitcast_fusion.5
  227.6 1.3 constant_dynamic-slice_fusion.6
  228.9 3.0 bitcast_reduce_fusion.2
  231.9 3.7 %fusion.48 = f32[4,8,128]{2,1,0:T(8,128)S(1)} fusion(f32[4,1024,128,8]{2,1,3,0:T(8,128)S(1)} %get-tuple-element.117, f32[4,8,128]{2,1,0:T(8,128)S(1)} %get-tuple-element.118, pred[4,1024]{1,0:T(4,128)(4,1)S(1)} %dynamic-slice_bitcast_fusion.4), kind=kLoop, calls=%fused_computation.7.clone.1 | loop fusion | flops 16773120 | bytes 16814080 | tf_op jit(solution)/shard_map/while/body/eval_jaxpr/reduce_sum | solution.py:45
  235.7 4.9 %fusion.49 = bf16[1,4,128,8,128]{2,4,3,1,0:T(8,128)(2,1)S(1)} fusion(f32[4,1024,128,8]{2,1,3,0:T(8,128)S(1)} %get-tuple-element.117, f32[4,8,128]{2,1,0:T(8,128)S(1)} %get-tuple-element.118, pred[4,1024]{1,0:T(4,128)(4,1)S(1)} %dynamic-slice_bitcast_fusion.4, bf16[4,1024,256]{2,1,0:T(8,128)(2,1)S(1)} %dynamic-slice_bitcast_fusion.5, ...), kind=kOutput, calls=%fused_computation.14.clone.1 | convolution fusion | flops 1091567616 | bytes 18911232 | tf_op jit(solution)/shard_map/while/body/eval_jaxpr/pgts,psd->ptgd/dot_general | solution.py:47
  240.6 0.7 copy.94
  241.3 1.0 constant_dynamic-update-slice_fusion.5
  242.4 1.7 dynamic-slice_bitcast_fusion.5
  244.1 1.3 constant_dynamic-slice_fusion.6
  245.4 3.0 bitcast_reduce_fusion.2
  248.5 3.7 %fusion.48 = f32[4,8,128]{2,1,0:T(8,128)S(1)} fusion(f32[4,1024,128,8]{2,1,3,0:T(8,128)S(1)} %get-tuple-element.117, f32[4,8,128]{2,1,0:T(8,128)S(1)} %get-tuple-element.118, pred[4,1024]{1,0:T(4,128)(4,1)S(1)} %dynamic-slice_bitcast_fusion.4), kind=kLoop, calls=%fused_computation.7.clone.1 | loop fusion | flops 16773120 | bytes 16814080 | tf_op jit(solution)/shard_map/while/body/eval_jaxpr/reduce_sum | solution.py:45
  252.2 4.9 %fusion.49 = bf16[1,4,128,8,128]{2,4,3,1,0:T(8,128)(2,1)S(1)} fusion(f32[4,1024,128,8]{2,1,3,0:T(8,128)S(1)} %get-tuple-element.117, f32[4,8,128]{2,1,0:T(8,128)S(1)} %get-tuple-element.118, pred[4,1024]{1,0:T(4,128)(4,1)S(1)} %dynamic-slice_bitcast_fusion.4, bf16[4,1024,256]{2,1,0:T(8,128)(2,1)S(1)} %dynamic-slice_bitcast_fusion.5, ...), kind=kOutput, calls=%fused_computation.14.clone.1 | convolution fusion | flops 1091567616 | bytes 18911232 | tf_op jit(solution)/shard_map/while/body/eval_jaxpr/pgts,psd->ptgd/dot_general | solution.py:47
  257.2 0.7 copy.94
  257.9 1.0 constant_dynamic-update-slice_fusion.5
  258.9 1.7 dynamic-slice_bitcast_fusion.5
  260.7 1.3 constant_dynamic-slice_fusion.6
  262.0 3.0 bitcast_reduce_fusion.2
  265.0 3.7 %fusion.48 = f32[4,8,128]{2,1,0:T(8,128)S(1)} fusion(f32[4,1024,128,8]{2,1,3,0:T(8,128)S(1)} %get-tuple-element.117, f32[4,8,128]{2,1,0:T(8,128)S(1)} %get-tuple-element.118, pred[4,1024]{1,0:T(4,128)(4,1)S(1)} %dynamic-slice_bitcast_fusion.4), kind=kLoop, calls=%fused_computation.7.clone.1 | loop fusion | flops 16773120 | bytes 16814080 | tf_op jit(solution)/shard_map/while/body/eval_jaxpr/reduce_sum | solution.py:45
  268.8 5.0 %fusion.49 = bf16[1,4,128,8,128]{2,4,3,1,0:T(8,128)(2,1)S(1)} fusion(f32[4,1024,128,8]{2,1,3,0:T(8,128)S(1)} %get-tuple-element.117, f32[4,8,128]{2,1,0:T(8,128)S(1)} %get-tuple-element.118, pred[4,1024]{1,0:T(4,128)(4,1)S(1)} %dynamic-slice_bitcast_fusion.4, bf16[4,1024,256]{2,1,0:T(8,128)(2,1)S(1)} %dynamic-slice_bitcast_fusion.5, ...), kind=kOutput, calls=%fused_computation.14.clone.1 | convolution fusion | flops 1091567616 | bytes 18911232 | tf_op jit(solution)/shard_map/while/body/eval_jaxpr/pgts,psd->ptgd/dot_general | solution.py:47
  273.7 0.7 copy.94
  274.5 1.0 constant_dynamic-update-slice_fusion.5
  275.5 1.7 dynamic-slice_bitcast_fusion.5
  277.2 1.3 constant_dynamic-slice_fusion.6
  278.5 3.0 bitcast_reduce_fusion.2
  281.6 3.7 %fusion.48 = f32[4,8,128]{2,1,0:T(8,128)S(1)} fusion(f32[4,1024,128,8]{2,1,3,0:T(8,128)S(1)} %get-tuple-element.117, f32[4,8,128]{2,1,0:T(8,128)S(1)} %get-tuple-element.118, pred[4,1024]{1,0:T(4,128)(4,1)S(1)} %dynamic-slice_bitcast_fusion.4), kind=kLoop, calls=%fused_computation.7.clone.1 | loop fusion | flops 16773120 | bytes 16814080 | tf_op jit(solution)/shard_map/while/body/eval_jaxpr/reduce_sum | solution.py:45
  285.3 5.0 %fusion.49 = bf16[1,4,128,8,128]{2,4,3,1,0:T(8,128)(2,1)S(1)} fusion(f32[4,1024,128,8]{2,1,3,0:T(8,128)S(1)} %get-tuple-element.117, f32[4,8,128]{2,1,0:T(8,128)S(1)} %get-tuple-element.118, pred[4,1024]{1,0:T(4,128)(4,1)S(1)} %dynamic-slice_bitcast_fusion.4, bf16[4,1024,256]{2,1,0:T(8,128)(2,1)S(1)} %dynamic-slice_bitcast_fusion.5, ...), kind=kOutput, calls=%fused_computation.14.clone.1 | convolution fusion | flops 1091567616 | bytes 18911232 | tf_op jit(solution)/shard_map/while/body/eval_jaxpr/pgts,psd->ptgd/dot_general | solution.py:47
  290.3 0.7 copy.94
  291.0 1.0 constant_dynamic-update-slice_fusion.5
  292.1 7.3 %all_to_all.69 = bf16[4,512,1024]{2,1,0:T(8,128)(2,1)} reshape(bf16[4,4,128,8,128]{4,3,2,1,0:T(8,128)(2,1)} %get-tuple-element.32) | data formatting | bytes 8388608 | tf_op jit(solution)/shard_map/all_to_all | solution.py:132
  299.4 54.3 %all_to_all.78 = bf16[4,512,1024]{2,1,0:T(8,128)(2,1)} all-to-all(bf16[4,512,1024]{2,1,0:T(8,128)(2,1)} %all_to_all.69), channel_id=1, replica_groups=mesh['seq'=64,'head'=4] {'head'}, dimensions={0} | all-to-all | bytes 8388608 | tf_op jit(solution)/shard_map/all_to_all | solution.py:132
  353.7 6.3 %copy.69 = bf16[512,4,1024]{0,2,1:T(8,128)(2,1)} copy(bf16[512,4,1024]{2,0,1:T(8,128)(2,1)} %bitcast.160) | data formatting | bytes 8388608 | tf_op jit(solution)/shard_map/all_to_all | solution.py:132
  359.9 6.4 %copy.70 = bf16[512,4096]{1,0:T(8,128)(2,1)} copy(bf16[512,4096]{0,1:T(8,128)(2,1)} %bitcast.161) | data formatting | bytes 8388608 | tf_op jit(solution)/shard_map/all_to_all | solution.py:132
  (49 shorter events, 2.5 us)
Async XLA Ops:
  6.5 1.0 copy-start
  6.5 17.8 %copy-start.2 = (s32[2]{0:T(128)S(1)}, s32[2]{0:T(128)}, u32[]{:S(2)}) copy-start(s32[2]{0:T(128)} %param.11) | copy-start | bytes 28
  8.5 12.3 %all-to-all-start = ((bf16[512,4,128]{2,0,1:T(8,128)(2,1)}), bf16[512,4,128]{2,0,1:T(8,128)(2,1)S(1)}, u32[]{:S(2)}, u32[]{:S(2)}) async-start(bf16[512,4,128]{2,0,1:T(8,128)(2,1)} %copy_bitcast_fusion.4), calls=%async_computation | async-start | bytes 1048576 | tf_op jit(solution)/shard_map/all_to_all | solution.py:55
  20.8 10.4 %all-to-all-start.1 = ((bf16[512,4,128]{2,0,1:T(8,128)(2,1)}), bf16[512,4,128]{2,0,1:T(8,128)(2,1)S(1)}, u32[]{:S(2)}, u32[]{:S(2)}) async-start(bf16[512,4,128]{2,0,1:T(8,128)(2,1)} %copy_bitcast_fusion.3), calls=%async_computation.1 | async-start | bytes 1048576 | tf_op jit(solution)/shard_map/all_to_all | solution.py:56
  24.2 101.6 %all-gather.5.cloned.1.call-start = ((), (), s32[]{:S(2)}) async-start(), calls=%async_computation.6 | async-start | bytes 4259840 | tf_op jit(solution)/shard_map/all_gather | solution.py:32
  36.6 49.8 %all-to-all-start.3 = ((bf16[512,4,1024]{2,0,1:T(8,128)(2,1)}), bf16[512,4,1024]{2,0,1:T(8,128)(2,1)}, u32[]{:S(2)}, u32[]{:S(2)}) async-start(bf16[512,4,1024]{2,0,1:T(8,128)(2,1)} %bitcast.159), calls=%async_computation.3 | async-start | bytes 8388608 | tf_op jit(solution)/shard_map/all_to_all | solution.py:54
  41.5 173.5 %all-gather.3.cloned.1.call-start = ((), (), s32[]{:S(2)}) async-start(), calls=%async_computation.5 | async-start | bytes 4259840 | tf_op jit(solution)/shard_map/all_gather | solution.py:32
  86.3 131.1 %all-to-all-start.2 = ((bf16[64,1,128,256]{3,2,1,0:T(8,128)(2,1)}), bf16[64,1,128,256]{3,2,1,0:T(8,128)(2,1)}, u32[]{:S(2)}, u32[]{:S(2)}) async-start(bf16[64,1,128,256]{3,2,1,0:T(8,128)(2,1)} %fusion.16), calls=%async_computation.2 | async-start | bytes 8388608 | tf_op jit(solution)/shard_map/all_to_all | solution.py:93
  105.5 9.0 %collective-permute-start = (bf16[128,256]{1,0:T(8,128)(2,1)S(1)}, bf16[128,256]{1,0:T(8,128)(2,1)S(1)}, u32[]{:S(2)}, u32[]{:S(2)}) collective-permute-start(bf16[128,256]{1,0:T(8,128)(2,1)S(1)} %get-tuple-element.79), channel_id=1, source_target_pairs={{0,4},{4,8},{8,12},{12,16},{16,20},{20,24},{24,28},{28,32},{32,36}... | collective-permute-start | bytes 196616 | tf_op jit(solution)/shard_map/ppermute | solution.py:22
  109.0 8.1 %collective-permute-start.1 = (bf16[128,256]{1,0:T(8,128)(2,1)S(1)}, bf16[128,256]{1,0:T(8,128)(2,1)S(1)}, u32[]{:S(2)}, u32[]{:S(2)}) collective-permute-start(bf16[128,256]{1,0:T(8,128)(2,1)S(1)} %get-tuple-element.78), channel_id=1, source_target_pairs={{4,0},{8,4},{12,8},{16,12},{20,16},{24,20},{28,24},{32,28},{36,32}... | collective-permute-start | bytes 196616 | tf_op jit(solution)/shard_map/ppermute | solution.py:24
  359.9 6.4 %copy-start.1 = (bf16[512,512]{1,0:T(8,128)(2,1)S(1)}, bf16[512,512]{1,0:T(8,128)(2,1)}, u32[]{:S(2)}) copy-start(bf16[512,512]{1,0:T(8,128)(2,1)} %param.8) | copy-start | bytes 1572868
Sparse Core Ops, SparseCore 0:
  32.0 88.4 all-gather.4
  123.2 91.6 all-gather.2
where the time goes:
time: 375 us; the launch traced here: 373 us
  waiting for transfers between devices  137 us (37%)
  local copies, waits for them, and re-layouts  72.7 us (19%)
  blocking collectives  54.3 us (14%)
  starting transfers between devices  36.7 us (10%)
  matrix products  31.9 us (9%)
  other arithmetic  22.1 us (6%)
  between operations  18.8 us (5%)
    all_gather x2, waiting for transfers between devices, picked(): lax.all_gather(shard, axis)  88.3 us
    all_to_all x1, blocking collectives, on_device(): lax.all_to_all(output_rows, 'head', split_axis=0, concat_axis=1, tiled=True)  54.3 us
    all_to_all x1, waiting for transfers between devices, on_device(): lax.all_to_all(query_rows, 'head', split_axis=1, concat_axis=0, tiled=True)  35.6 us
    all_to_all x3, local copies, waits for them, and re-layouts, on_device(): lax.all_to_all(output_rows, 'head', split_axis=0, concat_axis=1, tiled=True)  20 us
    dot_general x4, matrix products, attend_group(): jnp.einsum('pgts,psd->ptgd', rounded, values, preferred_element_type=jnp....  19.8 us
    all_to_all x1, starting transfers between devices, on_device(): lax.all_to_all(outgoing, 'seq', split_axis=0, concat_axis=0, tiled=True)  17.9 us
    reduce_sum x4, other arithmetic, attend_group(): row_total = jnp.sum(weights, axis=-1)  15 us
    dot_general x4, matrix products, attend_group(): jnp.einsum('ptgd,psd->pgts', query_group, key_part, preferred_element_typ...  12.1 us
  transfers between devices with their start and end apart: 8, of which 6 were waited for; matrix products, arithmetic and copies ran while one was open for 8% of the time, Pallas kernels for 0%

commit v1 on v0

v1 whole, which is shorter than its diff:
```python
import math

import jax
import jax.numpy as jnp
from jax import lax
from jax.experimental import pallas as pl
from jax.experimental.pallas import tpu as pltpu
from jax.sharding import PartitionSpec as P

BLOCK = 128
DIM = 128
GLOBALS = 2
RANDOM = 3
GROUP = 8
SCALE = 1.0 / math.sqrt(DIM)
NT = (((1,), (1,)), ((), ()))


def stacked(q_tile):
    return jnp.concatenate([q_tile[:, j * DIM : (j + 1) * DIM] for j in range(GROUP)], axis=0)


def near_kernel(edge, q, k0, k1, k2, v0, v1, v2, kg, vg, acc, stat):
    i = pl.program_id(0)
    rows = stacked(q[...])
    dot = lambda k: lax.dot_general(rows, k[...], NT, preferred_element_type=jnp.float32) * SCALE
    no_prev = jnp.logical_and(edge[0] == 1, i == 0)
    no_next = jnp.logical_and(edge[1] == 1, i == pl.num_programs(0) - 1)
    s0 = jnp.where(no_prev, -1e30, dot(k0))
    s2 = jnp.where(no_next, -1e30, dot(k2))
    scores = jnp.concatenate([s0, dot(k1), s2, dot(kg)], axis=1)
    top = jnp.max(scores, axis=1, keepdims=True)
    weights = jnp.exp(scores - top)
    total = jnp.sum(weights, axis=1, keepdims=True)
    values = jnp.concatenate([v0[...], v1[...], v2[...], vg[...]], axis=0)
    acc[...] = jnp.dot(weights.astype(jnp.bfloat16), values, preferred_element_type=jnp.float32)
    lane = lax.broadcasted_iota(jnp.int32, stat.shape, 1)
    stat[...] = jnp.where(lane < 64, top, total)


def far_kernel(q, kr, vr, acc, stat, out):
    rows = stacked(q[...])
    keys = kr[0].reshape(RANDOM * BLOCK, DIM)
    values = vr[0].reshape(RANDOM * BLOCK, DIM)
    scores = lax.dot_general(rows, keys, NT, preferred_element_type=jnp.float32) * SCALE
    top = stat[:, 0:1]
    total = stat[:, 64:65]
    peak = jnp.maximum(jnp.max(scores, axis=1, keepdims=True), top)
    weights = jnp.exp(scores - peak)
    shrink = jnp.exp(top - peak)
    total = total * shrink + jnp.sum(weights, axis=1, keepdims=True)
    mixed = acc[...] * shrink + jnp.dot(
        weights.astype(jnp.bfloat16), values, preferred_element_type=jnp.float32
    )
    mixed = (mixed / total).astype(jnp.bfloat16)
    for j in range(GROUP):
        out[:, j * DIM : (j + 1) * DIM] = mixed[j * BLOCK : (j + 1) * BLOCK]


def on_device(query_rows, key_rows, value_rows, random_table, global_blocks):
    rows, width = query_rows.shape
    seq_count = lax.axis_size("seq")
    heads = lax.axis_size("head")
    seq_index = lax.axis_index("seq")
    head_index = lax.axis_index("head")
    here = rows // BLOCK
    run = here * heads
    linear = seq_index * heads + head_index
    devices = seq_count * heads

    split = lambda part: lax.all_to_all(part, "head", split_axis=1, concat_axis=0, tiled=True)
    run_keys = split(key_rows).reshape(run, BLOCK, DIM)
    run_values = split(value_rows).reshape(run, BLOCK, DIM)

    table_head = lax.dynamic_index_in_dim(random_table, head_index, 1, keepdims=False)
    refs = table_head.reshape(seq_count, run * RANDOM)
    sources = jnp.max(jnp.where(refs // run == seq_index, refs % run, 0), axis=1)
    mine = lax.dynamic_index_in_dim(refs, seq_index, 0, keepdims=False)
    owners = mine // run

    def fetch(blocks):
        sent = jnp.take(blocks, sources, axis=0)
        got = lax.all_to_all(sent, "seq", split_axis=0, concat_axis=0, tiled=True)
        named = jnp.take(got, owners, axis=0).reshape(heads, here * RANDOM, BLOCK, DIM)
        return lax.all_to_all(named, "head", split_axis=0, concat_axis=0, tiled=True)

    far_keys = fetch(run_keys)
    far_values = fetch(run_values)

    paired = jnp.concatenate([key_rows, value_rows], axis=1)
    axes = ("seq", "head")
    before = lax.ppermute(paired[rows - BLOCK :], axes, [(n, n + 1) for n in range(devices - 1)])
    after = lax.ppermute(paired[:BLOCK], axes, [(n + 1, n) for n in range(devices - 1)])
    local = paired.reshape(here, BLOCK, paired.shape[1])
    owned = jnp.take(local, global_blocks % here, axis=0)
    owned = jnp.where((global_blocks // here == linear)[:, None, None], owned, jnp.zeros_like(owned))
    shared = lax.psum(owned, axes).reshape(GLOBALS * BLOCK, paired.shape[1])
    wide = jnp.concatenate([before, paired, after], axis=0)

    tasks = here * heads
    lines = GROUP * BLOCK
    tile = lambda fn: pl.BlockSpec((BLOCK, DIM), fn)
    q_spec = pl.BlockSpec((BLOCK, GROUP * DIM), lambda i, h: (i, h))
    state_spec = pl.BlockSpec((lines, DIM), lambda i, h: (i * heads + h, 0))
    state = jax.ShapeDtypeStruct((tasks * lines, DIM), jnp.float32)
    edge = jnp.stack([linear == 0, linear == devices - 1]).astype(jnp.int32)
    acc, stat = pl.pallas_call(
        near_kernel,
        grid=(here, heads),
        out_shape=(state, state),
        in_specs=[pl.BlockSpec(memory_space=pltpu.SMEM), q_spec]
        + [tile(lambda i, h, o=o: (i + o, h)) for o in range(3)]
        + [tile(lambda i, h, o=o: (i + o, heads + h)) for o in range(3)]
        + [
            pl.BlockSpec((GLOBALS * BLOCK, DIM), lambda i, h: (0, h)),
            pl.BlockSpec((GLOBALS * BLOCK, DIM), lambda i, h: (0, heads + h)),
        ],
        out_specs=(state_spec, state_spec),
        cost_estimate=pl.CostEstimate(flops=6_000_000_000, bytes_accessed=24_000_000, transcendentals=0),
        name="near",
    )(edge, query_rows, wide, wide, wide, wide, wide, wide, shared, shared)
    far_spec = pl.BlockSpec((1, RANDOM, BLOCK, DIM), lambda i, h: (h, i, 0, 0))
    return pl.pallas_call(
        far_kernel,
        grid=(here, heads),
        out_shape=jax.ShapeDtypeStruct((rows, width), jnp.bfloat16),
        in_specs=[q_spec, far_spec, far_spec, state_spec, state_spec],
        out_specs=q_spec,
        cost_estimate=pl.CostEstimate(flops=4_000_000_000, bytes_accessed=24_000_000, transcendentals=0),
        name="far",
    )(query_rows, far_keys, far_values, acc, stat)


def solution(mesh):
    split = P(("seq", "head"), None)
    return jax.shard_map(
        on_device,
        mesh=mesh,
        in_specs=(split, split, split, P(), P()),
        out_specs=split,
        check_vma=False,
    )
```

time: 375 us -> 533 us (1.42)
  waiting for transfers between devices: 137 us -> 325 us
  Pallas kernels: 0 us -> 69 us
  local copies, waits for them, and re-layouts: 72.7 us -> 14.6 us
  matrix products: 31.9 us -> 0 us
  blocking collectives: 54.3 us -> 65.6 us
  other arithmetic: 22.1 us -> 11.2 us
    psum x0 -> x1, waiting for transfers between devices: none -> 235 us  [on_device(): shared = lax.psum(owned, axes).reshape(GLOBALS * BLOCK, paired.shape[1])]
    all_gather x2 -> x0, waiting for transfers between devices: 88.3 us -> none  [picked(): lax.all_gather(shard, axis)]
    pallas_call x0 -> x2, Pallas kernels: none -> 69 us  [the longest x1 41.5 us: on_device(): pl.pallas_call(far_kernel, grid=(here, heads), out_shape=jax.ShapeDtypeSt...]
    dot_general x8 -> x0, matrix products: 31.9 us -> none  [the longest x4 19.8 us: attend_group(): jnp.einsum('pgts,psd->ptgd', rounded, values, preferred_element_type=jnp....]
    all_to_all x4 -> x5, waiting for transfers between devices: 43.5 us -> 75 us  [the longest x1 45.6 us: fetch(): got = lax.all_to_all(sent, 'seq', split_axis=0, concat_axis=0, tiled=True)]
    all_to_all x6 -> x2, local copies, waits for them, and re-layouts: 27.5 us -> 0.54 us  [on_device(): lax.all_to_all(part, 'head', split_axis=1, concat_axis=0, tiled=True)]
    reduce_sum x6 -> x0, other arithmetic: 15.2 us -> none  [the longest x4 15 us: attend_group(): row_total = jnp.sum(weights, axis=-1)]
    all_to_all x1, blocking collectives: 54.3 us -> 65.6 us  [fetch(): got = lax.all_to_all(sent, 'seq', split_axis=0, concat_axis=0, tiled=True)]
  transfers between devices with their start and end apart: 8 -> 8, of which waited for: 6 -> 6; matrix products, arithmetic and copies ran while one was open for 8% -> 2% of each run, Pallas kernels for 0% -> 5%
where the time goes in v1:
time: 533 us; the launch traced here: 531 us
  waiting for transfers between devices  325 us (61%)
  Pallas kernels  69 us (13%)
  blocking collectives  65.6 us (12%)
  starting transfers between devices  32.9 us (6%)
  local copies, waits for them, and re-layouts  14.6 us (3%)
  between operations  13.6 us (3%)
  other arithmetic  11.2 us (2%)
    psum x1, waiting for transfers between devices, on_device(): shared = lax.psum(owned, axes).reshape(GLOBALS * BLOCK, paired.shape[1])  235 us
    all_to_all x1, blocking collectives, fetch(): got = lax.all_to_all(sent, 'seq', split_axis=0, concat_axis=0, tiled=True)  65.6 us
    all_to_all x1, waiting for transfers between devices, fetch(): got = lax.all_to_all(sent, 'seq', split_axis=0, concat_axis=0, tiled=True)  45.6 us
    pallas_call x1, Pallas kernels, on_device(): pl.pallas_call(far_kernel, grid=(here, heads), out_shape=jax.ShapeDtypeSt...  41.5 us
    pallas_call x1, Pallas kernels, on_device(): pl.pallas_call(near_kernel, grid=(here, heads), out_shape=(state, state),...  27.4 us
    all_to_all x2, waiting for transfers between devices, fetch(): lax.all_to_all(named, 'head', split_axis=0, concat_axis=0, tiled=True)  17.5 us
    ppermute x1, waiting for transfers between devices, on_device(): lax.ppermute(paired[rows - BLOCK:], axes, [(n, n + 1) for n in range(devi...  14.9 us
    all_to_all x2, waiting for transfers between devices, on_device(): lax.all_to_all(part, 'head', split_axis=1, concat_axis=0, tiled=True)  11.9 us
  transfers between devices with their start and end apart: 8, of which 6 were waited for; matrix products, arithmetic and copies ran while one was open for 2% of the time, Pallas kernels for 5%

profile of v1, /device:TPU:1, one launch (start us, length us, event | category | flops | bytes accessed | tf_op | source)
XLA Modules:
  0.0 531.4 jit_solution(1453720172137401981)
XLA Ops:
  6.5 0.0 copy-start.2
  6.5 0.0 copy-start.3
  6.5 2.1 copy.8
  8.7 4.8 all-to-all-start
  13.5 0.9 fusion
  14.4 0.1 reduce_max.14
  14.5 0.0 copy-done.2
  14.5 1.0 copy.10
  15.5 0.1 reduce_max.18
  15.6 0.0 copy-done.3
  15.6 5.3 %all-to-all-done = bf16[512,4,128]{0,2,1:T(8,128)(2,1)S(1)} async-done(((bf16[512,4,128]{0,2,1:T(8,128)(2,1)}), bf16[512,4,128]{0,2,1:T(8,128)(2,1)S(1)}, u32[]{:S(2)}, u32[]{:S(2)}) %all-to-all-start) | async-done | bytes 524320 | tf_op jit(solution)/shard_map/all_to_all | solution.py:71
  21.0 3.5 all-to-all-start.3
  24.5 0.3 copy.9
  24.8 6.6 %all-to-all-done.3 = bf16[512,4,128]{0,2,1:T(8,128)(2,1)S(1)} async-done(((bf16[512,4,128]{0,2,1:T(8,128)(2,1)}), bf16[512,4,128]{0,2,1:T(8,128)(2,1)S(1)}, u32[]{:S(2)}, u32[]{:S(2)}) %all-to-all-start.3) | async-done | bytes 524320 | tf_op jit(solution)/shard_map/all_to_all | solution.py:71
  31.3 0.3 copy.11
  31.6 1.0 gather_fusion.3
  32.6 2.1 gather_fusion.1
  34.7 3.3 broadcast_select_fusion
  38.1 65.6 %all_to_all.52 = bf16[64,128,128]{2,1,0:T(8,128)(2,1)} all-to-all(bf16[64,128,128]{2,1,0:T(8,128)(2,1)S(1)} %get-tuple-element.22), channel_id=1, replica_groups=mesh['seq'=64,'head'=4] {'seq'}, dimensions={0} | all-to-all | bytes 4194304 | tf_op jit(solution)/shard_map/all_to_all | solution.py:83
  103.7 7.0 %all-to-all-start.1 = ((bf16[64,128,128]{2,1,0:T(8,128)(2,1)}), bf16[64,128,128]{2,1,0:T(8,128)(2,1)S(1)}, u32[]{:S(2)}, u32[]{:S(2)}) async-start(bf16[64,128,128]{2,1,0:T(8,128)(2,1)} %get-tuple-element.23), calls=%async_computation.1 | async-start | bytes 4194304 | tf_op jit(solution)/shard_map/all_to_all | solution.py:83
  110.6 0.2 copy.7
  110.9 0.3 reshape.48
  111.2 3.5 gather_fusion.4
  114.7 45.6 %all-to-all-done.1 = bf16[64,128,128]{2,1,0:T(8,128)(2,1)S(1)} async-done(((bf16[64,128,128]{2,1,0:T(8,128)(2,1)}), bf16[64,128,128]{2,1,0:T(8,128)(2,1)S(1)}, u32[]{:S(2)}, u32[]{:S(2)}) %all-to-all-start.1) | async-done | bytes 2097184 | tf_op jit(solution)/shard_map/all_to_all | solution.py:83
  160.3 1.9 gather_fusion.2
  162.3 3.9 broadcast_select_fusion.2
  166.2 0.0 copy-start.1
  166.2 3.7 all-to-all-start.2
  169.9 0.0 copy-done.1
  169.9 0.1 constant_dynamic-update-slice_fusion.1
  170.0 1.1 constant_dynamic-update-slice_fusion
  171.1 17.5 %all-to-all-done.2.kr = bf16[4,12,128,128]{3,2,1,0:T(8,128)(2,1)S(1)} async-done(((bf16[4,12,128,128]{3,2,1,0:T(8,128)(2,1)}), bf16[4,12,128,128]{3,2,1,0:T(8,128)(2,1)S(1)}, u32[]{:S(2)}, u32[]{:S(2)}) %all-to-all-start.2) | async-done | bytes 1572896 | tf_op jit(solution)/shard_map/all_to_all | solution.py:85
  188.6 0.0 copy-start
  188.6 4.4 all-to-all-start.5
  192.9 0.0 all-reduce.2.cloned.1.call-start
  193.0 0.0 copy-done
  193.0 3.3 collective-permute-start
  196.3 6.2 %collective-permute-start.1 = (bf16[128,1024]{1,0:T(8,128)(2,1)S(1)}, bf16[128,1024]{1,0:T(8,128)(2,1)S(1)}, u32[]{:S(2)}, u32[]{:S(2)}) collective-permute-start(bf16[128,1024]{1,0:T(8,128)(2,1)S(1)} %get-tuple-element.18), channel_id=1, source_target_pairs={{1,0},{2,1},{3,2},{4,3},{5,4},{6,5},{7,6},{8,7},{9,8},{10,9},{11,1... | collective-permute-start | bytes 786440 | tf_op jit(solution)/shard_map/ppermute | solution.py:93
  202.6 0.6 gather_fusion
  203.2 0.9 select_select_fusion
  204.1 0.0 all-reduce.2.cloned.1.call-update
  204.1 0.6 add_convert_fusion.edge
  204.7 14.9 %collective-permute-done = bf16[128,1024]{1,0:T(8,128)(2,1)S(1)} collective-permute-done((bf16[128,1024]{1,0:T(8,128)(2,1)S(1)}, bf16[128,1024]{1,0:T(8,128)(2,1)S(1)}, u32[]{:S(2)}, u32[]{:S(2)}) %collective-permute-start) | collective-permute-done | bytes 262176 | tf_op jit(solution)/shard_map/ppermute | solution.py:92
  219.7 0.0 collective-permute-done.1
  219.7 1.3 pad_maximum_fusion.k0.k1.k2.v0.v1.v2
  221.0 234.6 %all-reduce.2.cloned.1.call-done.kg.vg = bf16[256,1024]{1,0:T(8,128)(2,1)} async-done(((bf16[256,1024]{1,0:T(8,128)(2,1)}), bf16[256,1024]{1,0:T(8,128)(2,1)}) %all-reduce.2.cloned.1.call-update) | async-done | bytes 524304 | tf_op jit(solution)/shard_map/psum | solution.py:97
  455.6 27.4 %near.1 = (f32[16384,128]{1,0:T(8,128)}, f32[16384,128]{1,0:T(8,128)}) custom-call(s32[2]{0:T(128)} %add_convert_fusion.edge, bf16[512,4096]{1,0:T(8,128)(2,1)} %q.3, bf16[768,1024]{1,0:T(8,128)(2,1)} %pad_maximum_fusion.k0.k1.k2.v0.v1.v2, bf16[768,1024]{1,0:T(8,128)(2,1)} %pad_maximum_fusion.k0.k1.k2.v0.v1.v2, ...), custom_call_target="tpu_custom_call" | custom-call | flops 6000000000 | bytes 24000000 | tf_op jit(solution)/shard_map/near/pallas_call | solution.py:107
  483.0 0.0 all-to-all-done.5.vr
  483.0 41.5 %far.1 = bf16[512,4096]{1,0:T(8,128)(2,1)} custom-call(bf16[512,4096]{1,0:T(8,128)(2,1)} %q.3, bf16[4,12,128,128]{3,2,1,0:T(8,128)(2,1)} %copy-done, bf16[4,12,128,128]{3,2,1,0:T(8,128)(2,1)} %all-to-all-done.5.vr, f32[16384,128]{1,0:T(8,128)} %get-tuple-element.9.acc, f32[16384,128]{1,0:T(8,128)} %get-tuple-element.10.stat), custom_call_target="tpu_custom_call" | custom-call | flops 4000000000 | bytes 24000000 | tf_op jit(solution)/shard_map/far/pallas_call | solution.py:123
  (7 shorter events, 0.1 us)
Async XLA Ops:
  6.5 7.9 %copy-start.2 = (bf16[512,512]{1,0:T(8,128)(2,1)S(1)}, bf16[512,512]{1,0:T(8,128)(2,1)}, u32[]{:S(2)}) copy-start(bf16[512,512]{1,0:T(8,128)(2,1)} %param.11) | copy-start | bytes 1572868
  6.5 9.1 %copy-start.3 = (s32[2]{0:T(128)S(1)}, s32[2]{0:T(128)}, u32[]{:S(2)}) copy-start(s32[2]{0:T(128)} %param.13) | copy-start | bytes 28
  8.7 12.3 %all-to-all-start = ((bf16[512,4,128]{0,2,1:T(8,128)(2,1)}), bf16[512,4,128]{0,2,1:T(8,128)(2,1)S(1)}, u32[]{:S(2)}, u32[]{:S(2)}) async-start(bf16[512,4,128]{0,2,1:T(8,128)(2,1)} %bitcast.1), calls=%async_computation | async-start | bytes 1048576 | tf_op jit(solution)/shard_map/all_to_all | solution.py:71
  21.0 10.4 %all-to-all-start.3 = ((bf16[512,4,128]{0,2,1:T(8,128)(2,1)}), bf16[512,4,128]{0,2,1:T(8,128)(2,1)S(1)}, u32[]{:S(2)}, u32[]{:S(2)}) async-start(bf16[512,4,128]{0,2,1:T(8,128)(2,1)} %bitcast.5), calls=%async_computation.3 | async-start | bytes 1048576 | tf_op jit(solution)/shard_map/all_to_all | solution.py:71
  103.7 56.7 %all-to-all-start.1 = ((bf16[64,128,128]{2,1,0:T(8,128)(2,1)}), bf16[64,128,128]{2,1,0:T(8,128)(2,1)S(1)}, u32[]{:S(2)}, u32[]{:S(2)}) async-start(bf16[64,128,128]{2,1,0:T(8,128)(2,1)} %get-tuple-element.23), calls=%async_computation.1 | async-start | bytes 4194304 | tf_op jit(solution)/shard_map/all_to_all | solution.py:83
  166.2 3.7 copy-start.1
  166.2 22.4 %all-to-all-start.2 = ((bf16[4,12,128,128]{3,2,1,0:T(8,128)(2,1)}), bf16[4,12,128,128]{3,2,1,0:T(8,128)(2,1)S(1)}, u32[]{:S(2)}, u32[]{:S(2)}) async-start(bf16[4,12,128,128]{3,2,1,0:T(8,128)(2,1)} %bitcast.29), calls=%async_computation.2 | async-start | bytes 3145728 | tf_op jit(solution)/shard_map/all_to_all | solution.py:85
  188.6 4.5 copy-start
  188.6 294.4 %all-to-all-start.5 = ((bf16[4,12,128,128]{3,2,1,0:T(8,128)(2,1)}), bf16[4,12,128,128]{3,2,1,0:T(8,128)(2,1)}, u32[]{:S(2)}, u32[]{:S(2)}) async-start(bf16[4,12,128,128]{3,2,1,0:T(8,128)(2,1)} %bitcast.28), calls=%async_computation.5 | async-start | bytes 3145728 | tf_op jit(solution)/shard_map/all_to_all | solution.py:85
  192.9 262.6 %all-reduce.2.cloned.1.call-start = ((), (), s32[]{:S(2)}) async-start(), calls=%async_computation.6 | async-start | bytes 1048576 | tf_op jit(solution)/shard_map/psum | solution.py:97
  193.0 26.6 %collective-permute-start = (bf16[128,1024]{1,0:T(8,128)(2,1)S(1)}, bf16[128,1024]{1,0:T(8,128)(2,1)S(1)}, u32[]{:S(2)}, u32[]{:S(2)}) collective-permute-start(bf16[128,1024]{1,0:T(8,128)(2,1)S(1)} %get-tuple-element.17), channel_id=1, source_target_pairs={{0,1},{1,2},{2,3},{3,4},{4,5},{5,6},{6,7},{7,8},{8,9},{9,10},{10,1... | collective-permute-start | bytes 786440 | tf_op jit(solution)/shard_map/ppermute | solution.py:92
  196.3 23.4 %collective-permute-start.1 = (bf16[128,1024]{1,0:T(8,128)(2,1)S(1)}, bf16[128,1024]{1,0:T(8,128)(2,1)S(1)}, u32[]{:S(2)}, u32[]{:S(2)}) collective-permute-start(bf16[128,1024]{1,0:T(8,128)(2,1)S(1)} %get-tuple-element.18), channel_id=1, source_target_pairs={{1,0},{2,1},{3,2},{4,3},{5,4},{6,5},{7,6},{8,7},{9,8},{10,9},{11,1... | collective-permute-start | bytes 786440 | tf_op jit(solution)/shard_map/ppermute | solution.py:93
Sparse Core Ops, SparseCore 0:
  204.2 251.2 all-reduce.1

commit v2 on v1

v2 whole, which is shorter than its diff:
```python
import math

import jax
import jax.numpy as jnp
from jax import lax
from jax.experimental import pallas as pl
from jax.experimental.pallas import tpu as pltpu
from jax.sharding import PartitionSpec as P

BLOCK = 128
DIM = 128
GLOBALS = 2
RANDOM = 3
GROUP = 8
HALF = 4
SCALE = 1.0 / math.sqrt(DIM)
NT = (((1,), (1,)), ((), ()))
MESH = pl.DeviceIdType.MESH

ZS, YS, CS, XS = 8, 4, 2, 4
PLANE = YS * CS
HERE = 4
RUN = HERE * XS
NAMED = HERE * RANDOM
TASKS = HERE * XS
LINES = GROUP * BLOCK
PIECE = BLOCK // PLANE

CHUNKS = ((0, 0, 64), (0, 64, 64), (1, 0, 64), (1, 64, 32), (1, 96, 32))
COUNT = len(CHUNKS)
KEYS = (0, 1)
VALUES = (2, 3, 4)
SPOT = {0: 0, 1: 1, 7: 2, 2: 3, 6: 4, 3: 5, 5: 6, 4: 7}


def body(
    table, q_hbm, k_hbm, v_hbm, out_hbm,
    ring, outbox, inbox, named, given, probs, qbuf, kwin, vwin, acc, stat,
    gpart, gfrom, gring, gmine, gall,
    x1s, x1r, zs, zr, ys, yr, x2s, x2r, hs, hr,
    gbs, gbr, gcs, gcr, gds, gdr, ghs, ghr, local, outs,
):
    seq = lax.axis_index("seq")
    x = lax.axis_index("head")
    z, yc = seq // PLANE, seq % PLANE
    y, c = yc // CS, yc % CS
    linear = seq * XS + x
    total = ZS * PLANE * XS

    def in_plane(p):
        return lax.rem(y + p // CS, YS) * CS + lax.rem(c + p % CS, CS)

    def at_x(t):
        return lax.rem(x + t, XS)

    above = lax.rem(z + 1, ZS) * PLANE + yc
    below = lax.rem(z + ZS - 1, ZS) * PLANE + yc
    ahead = lax.rem(linear + 1, total)
    behind = lax.rem(linear + total - 1, total)
    ahead = (ahead // XS, lax.rem(ahead, XS))
    behind = (behind // XS, lax.rem(behind, XS))

    def remote(src, dst, send, recv, where):
        return pltpu.make_async_remote_copy(
            src_ref=src, dst_ref=dst, send_sem=send, recv_sem=recv,
            device_id=where, device_id_type=MESH,
        )

    def own_part(j):
        kind, first, size = CHUNKS[j]
        source = (k_hbm, v_hbm)[kind]
        columns = pl.ds(pl.multiple_of(x * DIM, DIM), DIM)
        return pltpu.make_async_copy(
            source.at[:, first : first + size, columns],
            ring[j][0].at[pl.ds(x * HERE, HERE)],
            local.at[j],
        )

    keep_k = pltpu.make_async_copy(k_hbm, kwin.at[1 : 1 + HERE], local.at[COUNT])
    keep_v = pltpu.make_async_copy(v_hbm, vwin.at[1 : 1 + HERE], local.at[COUNT + 1])
    keep_q = pltpu.make_async_copy(q_hbm, qbuf, local.at[COUNT + 2])

    barrier = pltpu.get_barrier_semaphore()
    partners = [(seq, at_x(t)) for t in range(1, XS)]
    partners += [(z * PLANE + in_plane(p), x) for p in range(1, PLANE)]
    partners += [(above, x), (below, x), ahead, behind]
    for partner in partners:
        pl.semaphore_signal(barrier, inc=1, device_id=partner, device_id_type=MESH)
    for j in range(COUNT):
        own_part(j).start()
    keep_k.start()
    keep_v.start()
    keep_q.start()
    pl.semaphore_wait(barrier, len(partners))

    def to_head(j, t):
        kind, first, size = CHUNKS[j]
        source = (k_hbm, v_hbm)[kind]
        columns = pl.ds(pl.multiple_of(at_x(t) * DIM, DIM), DIM)
        return remote(
            source.at[:, first : first + size, columns],
            ring[j][0].at[pl.ds(x * HERE, HERE)],
            x1s.at[j, t - 1], x1r.at[j, t - 1], (seq, at_x(t)),
        )

    for j in range(COUNT):
        for t in range(1, XS):
            to_head(j, t).start()
    sides = [
        remote(k_hbm.at[HERE - 1], kwin.at[0], hs.at[0], hr.at[0], ahead),
        remote(v_hbm.at[HERE - 1], vwin.at[0], hs.at[1], hr.at[1], ahead),
        remote(k_hbm.at[0], kwin.at[HERE + 1], hs.at[2], hr.at[2], behind),
        remote(v_hbm.at[0], vwin.at[HERE + 1], hs.at[3], hr.at[3], behind),
    ]
    for side in sides:
        side.start()

    def hop(j, way, step):
        before, after = step - 1, step
        if way:
            before, after = (ZS - before) % ZS, ZS - after
        src, dst = ring[j][before], ring[j][after]
        if step == ZS // 2:
            cut = slice(RUN // 2, RUN) if way else slice(0, RUN // 2)
            src, dst = src.at[cut], dst.at[cut]
        return remote(
            src, dst, zs.at[j, way, step - 1], zr.at[j, way, step - 1],
            (below if way else above, x),
        )

    def choose(j, d):
        size = CHUNKS[j][2]
        for p in range(PLANE):
            block = ring[j][d][table[d * PLANE + in_plane(p)]]
            if p:
                outbox[j][p - 1, SPOT[d]] = block
            else:
                inbox[j][SPOT[d]] = block

    def post(j, low, high):
        for p in range(1, PLANE):
            remote(
                outbox[j].at[p - 1, low:high],
                inbox[j].at[p * ZS + low : p * ZS + high],
                ys.at[j], yr.at[j], (z * PLANE + in_plane(p), x),
            ).start()

    def ring_start(j):
        own_part(j).wait()
        for t in range(1, XS):
            to_head(j, t).wait_recv()
        hop(j, 0, 1).start()
        hop(j, 1, 1).start()
        choose(j, 0)

    def ring_step(j, step):
        hop(j, 0, step).wait_recv()
        hop(j, 1, step).wait_recv()
        if step < ZS // 2:
            hop(j, 0, step + 1).start()
            hop(j, 1, step + 1).start()
            choose(j, step)
            choose(j, ZS - step)
            low = 0 if step == 1 else 2 * step - 1
            post(j, low, 2 * step + 1)
        else:
            choose(j, step)
            post(j, ZS - 1, ZS)

    def give(j, t):
        return remote(
            named[j].at[t - 1], given[j].at[t], x2s.at[j, t - 1], x2r.at[j, t - 1],
            (seq, at_x(t)),
        )

    def hand_out(j):
        whole = inbox[j].at[ZS : PLANE * ZS]
        pltpu.make_async_copy(whole, whole, yr.at[j]).wait()
        for t in [1, 2, 3, 0]:
            base = PLANE * ZS + at_x(t) * NAMED

            def entry(e, carry):
                block = inbox[j][table[base + e]]
                if t:
                    named[j][t - 1, e] = block
                else:
                    given[j][0, e] = block
                return carry

            lax.fori_loop(0, NAMED, entry, 0)
            if t:
                give(j, t).start()

    def take(j):
        for t in range(1, XS):
            give(j, t).wait_recv()

    tail = PLANE * ZS + XS * NAMED

    def split_globals():
        for g in range(GLOBALS):
            block = table[tail + g]
            for j in range(COUNT):
                kind, first, size = CHUNKS[j]
                rows = ring[j][0][block]
                for a in range(size // PIECE):
                    gpart[first // PIECE + a, g, kind] = rows[a * PIECE : (a + 1) * PIECE]
        gfrom[0] = gpart[yc]
        for p in range(1, PLANE):
            there = in_plane(p)
            remote(
                gpart.at[there], gfrom.at[p], gbs, gbr, (z * PLANE + there, x)
            ).start()

    def hop_globals(n):
        if n < 4:
            return remote(gring.at[n], gring.at[n + 1], gcs.at[n], gcr.at[n], (above, x))
        before = (ZS - (n - 4)) % ZS
        return remote(
            gring.at[before], gring.at[ZS - (n - 3)], gcs.at[n], gcr.at[n], (below, x)
        )

    def ring_globals():
        whole = gfrom.at[1:PLANE]
        pltpu.make_async_copy(whole, whole, gbr).wait()
        for g in range(GLOBALS):
            gring[0, g] = gfrom[table[tail + GLOBALS + g], g]
        hop_globals(0).start()
        hop_globals(4).start()

    def pass_globals(n):
        hop_globals(n).wait_recv()
        if n not in (3, 6):
            hop_globals(n + 1).start()

    def join_globals():
        for g in range(GLOBALS):
            piece = gring[table[tail + 2 * GLOBALS + g], g]
            gmine[g] = piece
            gall[0, yc, g] = piece
        for p in range(1, PLANE):
            remote(
                gmine, gall.at[0, yc], gds, gdr, (z * PLANE + in_plane(p), x)
            ).start()

    def widen(t):
        return remote(gall.at[0], gall.at[t], ghs.at[t - 1], ghr.at[t - 1], (seq, at_x(t)))

    def spread_globals():
        whole = gfrom.at[1:PLANE]
        pltpu.make_async_copy(whole, whole, gdr).wait()
        for t in range(1, XS):
            widen(t).start()

    lane = lax.broadcasted_iota(jnp.int32, (HALF * BLOCK, DIM), 1)

    def place(n):
        i, t = n // XS, lax.rem(n, XS)
        return i, t, lax.rem(x + XS - t, XS)

    def queries(i, h, part):
        first = (h * GROUP + part * HALF) * DIM
        rows = pl.ds(pl.multiple_of(i * BLOCK, BLOCK), BLOCK)
        return jnp.concatenate(
            [
                qbuf[rows, pl.ds(pl.multiple_of(first + m * DIM, DIM), DIM)]
                for m in range(HALF)
            ],
            axis=0,
        )

    def near(n, carry):
        i, t, h = place(n)
        columns = pl.ds(pl.multiple_of(h * DIM, DIM), DIM)
        keys = kwin[pl.ds(i, 3), :, columns].reshape(3 * BLOCK, DIM)
        values = vwin[pl.ds(i, 3), :, columns].reshape(3 * BLOCK, DIM)
        no_prev = jnp.logical_and(linear == 0, i == 0)
        no_next = jnp.logical_and(linear == total - 1, i == HERE - 1)
        spot = lax.broadcasted_iota(jnp.int32, (1, 3 * BLOCK), 1)
        low = jnp.where(no_prev, BLOCK, 0)
        high = jnp.where(no_next, 2 * BLOCK, 3 * BLOCK)
        shut = jnp.where(jnp.logical_and(spot >= low, spot < high), 0.0, -1e30)
        for part in range(GROUP // HALF):
            lines = slice(part * HALF * BLOCK, (part + 1) * HALF * BLOCK)
            scores = lax.dot_general(
                queries(i, h, part), keys, NT, preferred_element_type=jnp.float32
            )
            scores = scores * SCALE + shut
            top = jnp.max(scores, axis=1, keepdims=True)
            weights = jnp.exp(scores - top)
            summed = jnp.sum(weights, axis=1, keepdims=True)
            acc[n, lines] = jnp.dot(
                weights.astype(jnp.bfloat16), values, preferred_element_type=jnp.float32
            )
            old = stat[lines]
            old = jnp.where(lane == 2 * n, top, old)
            stat[lines] = jnp.where(lane == 2 * n + 1, summed, old)
        return carry

    def far(n, carry):
        i, t, h = place(n)
        gk = jnp.concatenate(
            [gall[t, :, g, 0].reshape(BLOCK, DIM) for g in range(GLOBALS)], axis=0
        )
        gv = jnp.concatenate(
            [gall[t, :, g, 1].reshape(BLOCK, DIM) for g in range(GLOBALS)], axis=0
        )
        entries = pl.ds(i * RANDOM, RANDOM)
        parts = []
        for v in VALUES:
            first, size = CHUNKS[v][1:]
            source, offset = (given[0], first) if first < 64 else (given[1], first - 64)
            parts.append(
                source[t, entries, offset : offset + size, :].reshape(RANDOM * size, DIM)
            )
        for part in range(GROUP // HALF):
            lines = slice(part * HALF * BLOCK, (part + 1) * HALF * BLOCK)
            rows = queries(i, h, part)
            score = lambda keys: SCALE * lax.dot_general(
                rows, keys, NT, preferred_element_type=jnp.float32
            )
            shared = score(gk)
            scores = [score(keys) for keys in parts]
            old = stat[lines]
            top = jnp.sum(jnp.where(lane == 2 * n, old, 0.0), axis=1, keepdims=True)
            summed = jnp.sum(jnp.where(lane == 2 * n + 1, old, 0.0), axis=1, keepdims=True)
            peak = jnp.maximum(top, jnp.max(shared, axis=1, keepdims=True))
            for s in scores:
                peak = jnp.maximum(peak, jnp.max(s, axis=1, keepdims=True))
            shrink = jnp.exp(top - peak)
            weights = jnp.exp(shared - peak)
            summed = summed * shrink + jnp.sum(weights, axis=1, keepdims=True)
            acc[n, lines] = acc[n, lines] * shrink + jnp.dot(
                weights.astype(jnp.bfloat16), gv, preferred_element_type=jnp.float32
            )
            for m, s in enumerate(scores):
                weights = jnp.exp(s - peak)
                summed = summed + jnp.sum(weights, axis=1, keepdims=True)
                probs[m][n, lines] = weights.astype(jnp.bfloat16)
            stat[lines] = jnp.where(lane == 2 * n, 1.0 / summed, old)
        return carry

    def mix(m, n):
        i, t, h = place(n)
        j = VALUES[m]
        size = CHUNKS[j][2]
        values = given[j][t, pl.ds(i * RANDOM, RANDOM)].reshape(RANDOM * size, DIM)
        return i, h, jnp.dot(probs[m][n], values, preferred_element_type=jnp.float32)

    def middle(m):
        def step(n, carry):
            acc[n] = acc[n] + mix(m, n)[2]
            return carry

        return step

    def out_tile(i, h):
        rows = pl.ds(pl.multiple_of(i * BLOCK, BLOCK), BLOCK)
        columns = pl.ds(pl.multiple_of(h * GROUP * DIM, GROUP * DIM), GROUP * DIM)
        return pltpu.make_async_copy(qbuf.at[rows, columns], out_hbm.at[rows, columns], outs)

    def last(n, carry):
        i, h, mixed = mix(len(VALUES) - 1, n)
        wide = lax.broadcasted_iota(jnp.int32, (LINES, DIM), 1)
        scale = jnp.sum(jnp.where(wide == 2 * n, stat[...], 0.0), axis=1, keepdims=True)
        mixed = ((acc[n] + mixed) * scale).astype(jnp.bfloat16)
        rows = pl.ds(pl.multiple_of(i * BLOCK, BLOCK), BLOCK)
        for m in range(GROUP):
            columns = pl.ds(pl.multiple_of((h * GROUP + m) * DIM, DIM), DIM)
            qbuf[rows, columns] = mixed[m * BLOCK : (m + 1) * BLOCK]
        out_tile(i, h).start()
        return carry

    def some(fn, low, high):
        lax.fori_loop(low, high, fn, 0)

    a, b = KEYS
    ring_start(a)
    ring_start(b)
    keep_q.wait()
    keep_k.wait()
    keep_v.wait()
    for side in sides:
        side.wait_recv()
    some(near, 0, 3)
    ring_step(a, 1)
    some(near, 3, 6)
    for j in VALUES:
        own_part(j).wait()
        for t in range(1, XS):
            to_head(j, t).wait_recv()
    split_globals()
    ring_step(b, 1)
    some(near, 6, 9)
    ring_globals()
    ring_step(a, 2)
    some(near, 9, 12)
    pass_globals(0)
    pass_globals(4)
    ring_step(b, 2)
    some(near, 12, 14)
    pass_globals(1)
    pass_globals(5)
    ring_step(a, 3)
    some(near, 14, 16)
    pass_globals(2)
    pass_globals(6)
    ring_step(b, 3)
    pass_globals(3)
    join_globals()
    for j in VALUES:
        hop(j, 0, 1).start()
        hop(j, 1, 1).start()
    ring_step(a, 4)
    spread_globals()
    ring_step(b, 4)
    for j in VALUES:
        choose(j, 0)
    hand_out(a)
    ring_step(VALUES[0], 1)
    hand_out(b)
    ring_step(VALUES[1], 1)
    ring_step(VALUES[2], 1)
    ring_step(VALUES[0], 2)
    for t in range(1, XS):
        widen(t).wait_recv()
    take(a)
    take(b)
    ring_step(VALUES[1], 2)
    some(far, 0, 2)
    ring_step(VALUES[2], 2)
    some(far, 2, 5)
    ring_step(VALUES[0], 3)
    some(far, 5, 8)
    ring_step(VALUES[1], 3)
    some(far, 8, 10)
    ring_step(VALUES[2], 3)
    some(far, 10, 12)
    ring_step(VALUES[0], 4)
    some(far, 12, 14)
    hand_out(VALUES[0])
    ring_step(VALUES[1], 4)
    some(far, 14, 16)
    hand_out(VALUES[1])
    ring_step(VALUES[2], 4)
    take(VALUES[0])
    some(middle(0), 0, 8)
    hand_out(VALUES[2])
    some(middle(0), 8, 16)
    take(VALUES[1])
    some(middle(1), 0, 16)
    take(VALUES[2])
    some(last, 0, 16)

    for j in range(COUNT):
        for t in range(1, XS):
            to_head(j, t).wait_send()
            give(j, t).wait_send()
        for step in range(1, ZS // 2 + 1):
            hop(j, 0, step).wait_send()
            hop(j, 1, step).wait_send()
        pltpu.make_async_copy(outbox[j], outbox[j], ys.at[j]).wait()
    for side in sides:
        side.wait_send()
    whole = gfrom.at[1:PLANE]
    pltpu.make_async_copy(whole, whole, gbs).wait()
    pltpu.make_async_copy(whole, whole, gds).wait()
    for n in range(ZS - 1):
        hop_globals(n).wait_send()
    for t in range(1, XS):
        widen(t).wait_send()
    pltpu.make_async_copy(qbuf, out_hbm, outs).wait()


def on_device(query_rows, key_rows, value_rows, random_table, global_blocks):
    rows, width = query_rows.shape
    seq_count = lax.axis_size("seq")
    seq = lax.axis_index("seq")
    x = lax.axis_index("head")
    z, yc = seq // PLANE, seq % PLANE
    y, c = yc // CS, yc % CS

    refs = lax.dynamic_index_in_dim(random_table, x, 1, keepdims=False)
    refs = refs.reshape(seq_count, RUN * RANDOM)
    plane = lax.dynamic_slice_in_dim(refs, z * PLANE, PLANE, 0)
    up = jnp.arange(ZS, dtype=jnp.int32)
    senders = ((z - up) % ZS) * PLANE + yc
    wanted = jnp.max(
        jnp.where(plane[None] // RUN == senders[:, None, None], plane[None] % RUN, 0), axis=2
    )
    spots = jnp.array([SPOT[d] for d in range(ZS)], jnp.int32)

    def across(owner):
        other = owner % PLANE
        return ((y - other // CS) % YS) * CS + (c - other % CS) % CS

    mine = lax.dynamic_index_in_dim(plane, yc, 0, keepdims=False) // RUN
    up_of = lambda owner: (z - owner // PLANE) % ZS
    lies = across(mine) * ZS + jnp.sum(
        jnp.where(up_of(mine)[:, None] == up[None], spots[None], 0), axis=1
    )
    owners = global_blocks // RUN
    table = jnp.concatenate(
        [wanted.reshape(-1), lies, global_blocks % RUN, across(owners), up_of(owners)]
    )

    vmem = lambda *shape: pltpu.VMEM(shape, jnp.bfloat16)
    dma = pltpu.SemaphoreType.DMA
    sizes = [size for _, _, size in CHUNKS]
    scratch = [
        [[vmem(RUN, r, DIM) for _ in range(ZS)] for r in sizes],
        [vmem(PLANE - 1, ZS, r, DIM) for r in sizes],
        [vmem(PLANE * ZS, r, DIM) for r in sizes],
        [vmem(XS - 1, NAMED, r, DIM) for r in sizes],
        [vmem(XS, NAMED, r, DIM) for r in sizes],
        [vmem(TASKS, LINES, RANDOM * sizes[v]) for v in VALUES],
        vmem(rows, width),
        vmem(HERE + 2, BLOCK, XS * DIM),
        vmem(HERE + 2, BLOCK, XS * DIM),
        pltpu.VMEM((TASKS, LINES, DIM), jnp.float32),
        pltpu.VMEM((LINES, DIM), jnp.float32),
        vmem(PLANE, GLOBALS, 2, PIECE, DIM),
        vmem(PLANE, GLOBALS, 2, PIECE, DIM),
        vmem(ZS, GLOBALS, 2, PIECE, DIM),
        vmem(GLOBALS, 2, PIECE, DIM),
        vmem(XS, PLANE, GLOBALS, 2, PIECE, DIM),
        dma((COUNT, XS - 1)), dma((COUNT, XS - 1)),
        dma((COUNT, 2, ZS // 2)), dma((COUNT, 2, ZS // 2)),
        dma((COUNT,)), dma((COUNT,)),
        dma((COUNT, XS - 1)), dma((COUNT, XS - 1)),
        dma((4,)), dma((4,)),
        dma, dma, dma((ZS - 1,)), dma((ZS - 1,)), dma, dma, dma((XS - 1,)), dma((XS - 1,)),
        dma((COUNT + 3,)), dma,
    ]
    anywhere = pl.BlockSpec(memory_space=pl.ANY)
    blocks = lambda part: part.reshape(HERE, BLOCK, part.shape[1])
    return pl.pallas_call(
        body,
        out_shape=jax.ShapeDtypeStruct((rows, width), jnp.bfloat16),
        in_specs=[pl.BlockSpec(memory_space=pltpu.SMEM)] + [anywhere] * 3,
        out_specs=anywhere,
        scratch_shapes=scratch,
        compiler_params=pltpu.CompilerParams(
            collective_id=0, has_side_effects=True, vmem_limit_bytes=67_043_328
        ),
        name="attend",
    )(table, query_rows, blocks(key_rows), blocks(value_rows))


def solution(mesh):
    split = P(("seq", "head"), None)
    return jax.shard_map(
        on_device,
        mesh=mesh,
        in_specs=(split, split, split, P(), P()),
        out_specs=split,
        check_vma=False,
    )
```

time: 533 us -> 152 us (0.29)
  waiting for transfers between devices: 325 us -> 0 us
  Pallas kernels: 69 us -> 143 us
  blocking collectives: 65.6 us -> 0 us
  starting transfers between devices: 32.9 us -> 0 us
  between operations: 13.6 us -> 0.04 us
  other arithmetic: 11.2 us -> 1.84 us
  local copies, waits for them, and re-layouts: 14.6 us -> 6.67 us
    psum x1 -> x0, waiting for transfers between devices: 235 us -> none  [on_device(): shared = lax.psum(owned, axes).reshape(GLOBALS * BLOCK, paired.shape[1])]
    all_to_all x5 -> x0, waiting for transfers between devices: 75 us -> none  [the longest x1 45.6 us: fetch(): got = lax.all_to_all(sent, 'seq', split_axis=0, concat_axis=0, tiled=True)]
    pallas_call x2 -> x1, Pallas kernels: 69 us -> 143 us  [on_device(): pl.pallas_call(body, out_shape=jax.ShapeDtypeStruct((rows, width), jnp.bf...]
    all_to_all x1 -> x0, blocking collectives: 65.6 us -> none  [fetch(): got = lax.all_to_all(sent, 'seq', split_axis=0, concat_axis=0, tiled=True)]
    all_to_all x5 -> x0, starting transfers between devices: 23.3 us -> none  [the longest x2 8.3 us: on_device(): lax.all_to_all(part, 'head', split_axis=1, concat_axis=0, tiled=True)]
    ppermute x2 -> x0, waiting for transfers between devices: 15 us -> none  [the longest x1 14.9 us: on_device(): lax.ppermute(paired[rows - BLOCK:], axes, [(n, n + 1) for n in range(devi...]
    ppermute x2 -> x0, starting transfers between devices: 9.51 us -> none  [the longest x1 6.24 us: on_device(): lax.ppermute(paired[:BLOCK], axes, [(n + 1, n) for n in range(devices - 1)])]
    gather x5 -> x0, local copies, waits for them, and re-layouts: 9.15 us -> none  [the longest x2 5.48 us: fetch(): jnp.take(got, owners, axis=0).reshape(heads, here * RANDOM, BLOCK, DIM)]
  transfers between devices with their start and end apart: 8 -> 0, of which waited for: 6 -> 0; matrix products, arithmetic and copies ran while one was open for 2% -> 0% of each run, Pallas kernels for 5% -> 0%
where the time goes in v2:
time: 152 us
  Pallas kernels  143 us (94%)
  local copies, waits for them, and re-layouts  6.67 us (4%)
  other arithmetic  1.84 us (1%)
    pallas_call x1, Pallas kernels, on_device(): pl.pallas_call(body, out_shape=jax.ShapeDtypeStruct((rows, width), jnp.bf...  143 us
    unnamed x1, local copies, waits for them, and re-layouts  4.7 us

profile of v2, /device:TPU:1, one launch (start us, length us, event | category | flops | bytes accessed | tf_op | source)
XLA Modules:
  0.0 151.9 jit_solution(7846942725962930200)
XLA Ops:
  0.0 0.7 and_select_fusion
  0.7 0.8 constant_dynamic-slice_fusion.1
  1.5 0.2 copy.8
  1.8 0.3 reshape.112
  2.1 0.7 select_reduce_fusion.1
  2.9 0.3 select_reduce_fusion
  3.2 0.1 reshape.113
  3.2 0.6 concatenate.3.table
  3.8 143.3 %attend.1 = bf16[512,4096]{1,0:T(8,128)(2,1)} custom-call(s32[118]{0:T(128)} %concatenate.3.table, bf16[512,4096]{1,0:T(8,128)(2,1)} %q_hbm.1, bf16[4,128,512]{2,1,0:T(8,128)(2,1)} %bitcast.9, bf16[4,128,512]{2,1,0:T(8,128)(2,1)} %bitcast.10), custom_call_target="tpu_custom_call" | custom-call | tf_op jit(solution)/shard_map/attend/pallas_call | solution.py:537
  147.2 4.7 %copy.10 = bf16[512,4096]{1,0:T(8,128)(2,1)} copy(bf16[512,4096]{1,0:T(8,128)(2,1)} %attend.1) | data formatting | bytes 8388608
  (6 shorter events, 0.1 us)

commit v3 on v2

--- a/solution.py
+++ b/solution.py
@@ -26,16 +26,21 @@
 LINES = GROUP * BLOCK
 PIECE = BLOCK // PLANE
 
-CHUNKS = ((0, 0, 64), (0, 64, 64), (1, 0, 64), (1, 64, 32), (1, 96, 32))
+SIZE = 32
+CHUNKS = tuple((kind, first) for kind in (0, 1) for first in range(0, BLOCK, SIZE))
 COUNT = len(CHUNKS)
-KEYS = (0, 1)
-VALUES = (2, 3, 4)
+KEYS = range(COUNT // 2)
+VALUES = ((4, 5), (6,), (7,))
+REACH = 2
+SPAN = 2 * REACH + 1
+DEPTH = 12
+SLOTS = PLANE + PLANE // 2
 SPOT = {0: 0, 1: 1, 7: 2, 2: 3, 6: 4, 3: 5, 5: 6, 4: 7}
 
 
 def body(
-    table, q_hbm, k_hbm, v_hbm, out_hbm,
-    ring, outbox, inbox, named, given, probs, qbuf, kwin, vwin, acc, stat,
+    wanted, lies, shared_at, q_hbm, k_hbm, v_hbm, out_hbm,
+    ring, relay, slots, middle_slots, outbox, inbox, named, given, probs, qbuf, kwin, vwin, acc, stat,
     gpart, gfrom, gring, gmine, gall,
     x1s, x1r, zs, zr, ys, yr, x2s, x2r, hs, hr,
     gbs, gbr, gcs, gcr, gds, gdr, ghs, ghr, local, outs,
@@ -67,11 +72,11 @@
         )
 
     def own_part(j):
-        kind, first, size = CHUNKS[j]
+        kind, first = CHUNKS[j]
         source = (k_hbm, v_hbm)[kind]
         columns = pl.ds(pl.multiple_of(x * DIM, DIM), DIM)
         return pltpu.make_async_copy(
-            source.at[:, first : first + size, columns],
+            source.at[:, first : first + SIZE, columns],
             ring[j][0].at[pl.ds(x * HERE, HERE)],
             local.at[j],
         )
@@ -83,7 +88,8 @@
     barrier = pltpu.get_barrier_semaphore()
     partners = [(seq, at_x(t)) for t in range(1, XS)]
     partners += [(z * PLANE + in_plane(p), x) for p in range(1, PLANE)]
-    partners += [(above, x), (below, x), ahead, behind]
+    partners += [(lax.rem(z + n, ZS) * PLANE + yc, x) for n in range(1, ZS)]
+    partners += [ahead, behind]
     for partner in partners:
         pl.semaphore_signal(barrier, inc=1, device_id=partner, device_id_type=MESH)
     for j in range(COUNT):
@@ -94,11 +100,11 @@
     pl.semaphore_wait(barrier, len(partners))
 
     def to_head(j, t):
-        kind, first, size = CHUNKS[j]
+        kind, first = CHUNKS[j]
         source = (k_hbm, v_hbm)[kind]
         columns = pl.ds(pl.multiple_of(at_x(t) * DIM, DIM), DIM)
         return remote(
-            source.at[:, first : first + size, columns],
+            source.at[:, first : first + SIZE, columns],
             ring[j][0].at[pl.ds(x * HERE, HERE)],
             x1s.at[j, t - 1], x1r.at[j, t - 1], (seq, at_x(t)),
         )
@@ -116,22 +122,45 @@
         side.start()
 
     def hop(j, way, step):
-        before, after = step - 1, step
-        if way:
-            before, after = (ZS - before) % ZS, ZS - after
-        src, dst = ring[j][before], ring[j][after]
-        if step == ZS // 2:
-            cut = slice(RUN // 2, RUN) if way else slice(0, RUN // 2)
-            src, dst = src.at[cut], dst.at[cut]
+        if step <= REACH:
+            before, after = step - 1, step
+            if way:
+                before, after = (ZS - before) % ZS, ZS - after
+            src, dst = ring[j][before], ring[j][after]
+        elif step == REACH + 1:
+            src, dst = relay[j].at[way], slots[j].at[way]
+        else:
+            half = PLANE // 2
+            src = slots[j].at[way, PLANE:SLOTS]
+            dst = middle_slots[j].at[way * half : (way + 1) * half]
         return remote(
             src, dst, zs.at[j, way, step - 1], zr.at[j, way, step - 1],
             (below if way else above, x),
         )
 
+    def named_by(target, origin, place_in_plane):
+        return wanted[((target + REACH) * SPAN + origin + REACH) * PLANE + place_in_plane]
+
+    def prepare(j, way):
+        sign = -1 if way else 1
+        source = ring[j][ZS - REACH if way else REACH]
+        for r in range(PLANE):
+            relay[j][way, r] = source[named_by(sign, -REACH * sign, r)]
+        for r in range(PLANE // 2):
+            further = r + (PLANE // 2 if way else 0)
+            relay[j][way, PLANE + r] = source[named_by(2 * sign, -REACH * sign, further)]
+
     def choose(j, d):
-        size = CHUNKS[j][2]
         for p in range(PLANE):
-            block = ring[j][d][table[d * PLANE + in_plane(p)]]
+            there = in_plane(p)
+            if d <= REACH:
+                block = ring[j][d][named_by(0, -d, there)]
+            elif d >= ZS - REACH:
+                block = ring[j][d][named_by(0, ZS - d, there)]
+            elif d == ZS // 2:
+                block = middle_slots[j][there]
+            else:
+                block = slots[j][0 if d < ZS // 2 else 1, there]
             if p:
                 outbox[j][p - 1, SPOT[d]] = block
             else:
@@ -145,10 +174,17 @@
                 ys.at[j], yr.at[j], (z * PLANE + in_plane(p), x),
             ).start()
 
-    def ring_start(j):
+    ready = set()
+
+    def ring_ready(j):
+        if j in ready:
+            return
+        ready.add(j)
         own_part(j).wait()
         for t in range(1, XS):
             to_head(j, t).wait_recv()
+
+    def ring_start(j):
         hop(j, 0, 1).start()
         hop(j, 1, 1).start()
         choose(j, 0)
@@ -156,6 +192,9 @@
     def ring_step(j, step):
         hop(j, 0, step).wait_recv()
         hop(j, 1, step).wait_recv()
+        if step == REACH:
+            prepare(j, 0)
+            prepare(j, 1)
         if step < ZS // 2:
             hop(j, 0, step + 1).start()
             hop(j, 1, step + 1).start()
@@ -177,10 +216,10 @@
         whole = inbox[j].at[ZS : PLANE * ZS]
         pltpu.make_async_copy(whole, whole, yr.at[j]).wait()
         for t in [1, 2, 3, 0]:
-            base = PLANE * ZS + at_x(t) * NAMED
+            base = at_x(t) * NAMED
 
             def entry(e, carry):
-                block = inbox[j][table[base + e]]
+                block = inbox[j][lies[base + e]]
                 if t:
                     named[j][t - 1, e] = block
                 else:
@@ -195,15 +234,13 @@
         for t in range(1, XS):
             give(j, t).wait_recv()
 
-    tail = PLANE * ZS + XS * NAMED
-
     def split_globals():
         for g in range(GLOBALS):
-            block = table[tail + g]
+            block = shared_at[g]
             for j in range(COUNT):
-                kind, first, size = CHUNKS[j]
+                kind, first = CHUNKS[j]
                 rows = ring[j][0][block]
-                for a in range(size // PIECE):
+                for a in range(SIZE // PIECE):
                     gpart[first // PIECE + a, g, kind] = rows[a * PIECE : (a + 1) * PIECE]
         gfrom[0] = gpart[yc]
         for p in range(1, PLANE):
@@ -212,30 +249,23 @@
                 gpart.at[there], gfrom.at[p], gbs, gbr, (z * PLANE + there, x)
             ).start()
 
-    def hop_globals(n):
-        if n < 4:
-            return remote(gring.at[n], gring.at[n + 1], gcs.at[n], gcr.at[n], (above, x))
-        before = (ZS - (n - 4)) % ZS
-        return remote(
-            gring.at[before], gring.at[ZS - (n - 3)], gcs.at[n], gcr.at[n], (below, x)
-        )
+    def to_plane(n):
+        there = lax.rem(z + n, ZS) * PLANE + yc
+        return remote(gring.at[0], gring.at[n], gcs.at[n - 1], gcr.at[n - 1], (there, x))
 
     def ring_globals():
         whole = gfrom.at[1:PLANE]
         pltpu.make_async_copy(whole, whole, gbr).wait()
         for g in range(GLOBALS):
-            gring[0, g] = gfrom[table[tail + GLOBALS + g], g]
-        hop_globals(0).start()
-        hop_globals(4).start()
-
-    def pass_globals(n):
-        hop_globals(n).wait_recv()
-        if n not in (3, 6):
-            hop_globals(n + 1).start()
+            gring[0, g] = gfrom[shared_at[GLOBALS + g], g]
+        for n in range(1, ZS):
+            to_plane(n).start()
 
     def join_globals():
+        for n in range(1, ZS):
+            to_plane(n).wait_recv()
         for g in range(GLOBALS):
-            piece = gring[table[tail + 2 * GLOBALS + g], g]
+            piece = gring[shared_at[2 * GLOBALS + g], g]
             gmine[g] = piece
             gall[0, yc, g] = piece
         for p in range(1, PLANE):
@@ -306,46 +336,48 @@
             [gall[t, :, g, 1].reshape(BLOCK, DIM) for g in range(GLOBALS)], axis=0
         )
         entries = pl.ds(i * RANDOM, RANDOM)
-        parts = []
-        for v in VALUES:
-            first, size = CHUNKS[v][1:]
-            source, offset = (given[0], first) if first < 64 else (given[1], first - 64)
-            parts.append(
-                source[t, entries, offset : offset + size, :].reshape(RANDOM * size, DIM)
-            )
+        keys = jnp.concatenate(
+            [gk] + [given[j][t, entries].reshape(RANDOM * SIZE, DIM) for j in KEYS], axis=0
+        )
+        split = GLOBALS * BLOCK
         for part in range(GROUP // HALF):
             lines = slice(part * HALF * BLOCK, (part + 1) * HALF * BLOCK)
             rows = queries(i, h, part)
-            score = lambda keys: SCALE * lax.dot_general(
+            scores = SCALE * lax.dot_general(
                 rows, keys, NT, preferred_element_type=jnp.float32
             )
-            shared = score(gk)
-            scores = [score(keys) for keys in parts]
             old = stat[lines]
             top = jnp.sum(jnp.where(lane == 2 * n, old, 0.0), axis=1, keepdims=True)
             summed = jnp.sum(jnp.where(lane == 2 * n + 1, old, 0.0), axis=1, keepdims=True)
-            peak = jnp.maximum(top, jnp.max(shared, axis=1, keepdims=True))
-            for s in scores:
-                peak = jnp.maximum(peak, jnp.max(s, axis=1, keepdims=True))
+            peak = jnp.maximum(top, jnp.max(scores, axis=1, keepdims=True))
             shrink = jnp.exp(top - peak)
-            weights = jnp.exp(shared - peak)
+            weights = jnp.exp(scores - peak)
             summed = summed * shrink + jnp.sum(weights, axis=1, keepdims=True)
+            weights = weights.astype(jnp.bfloat16)
             acc[n, lines] = acc[n, lines] * shrink + jnp.dot(
-                weights.astype(jnp.bfloat16), gv, preferred_element_type=jnp.float32
+                weights[:, :split], gv, preferred_element_type=jnp.float32
             )
-            for m, s in enumerate(scores):
-                weights = jnp.exp(s - peak)
-                summed = summed + jnp.sum(weights, axis=1, keepdims=True)
-                probs[m][n, lines] = weights.astype(jnp.bfloat16)
+            probs[n, lines] = weights[:, split:]
             stat[lines] = jnp.where(lane == 2 * n, 1.0 / summed, old)
         return carry
 
     def mix(m, n):
         i, t, h = place(n)
-        j = VALUES[m]
-        size = CHUNKS[j][2]
-        values = given[j][t, pl.ds(i * RANDOM, RANDOM)].reshape(RANDOM * size, DIM)
-        return i, h, jnp.dot(probs[m][n], values, preferred_element_type=jnp.float32)
+        rows = RANDOM * SIZE
+        first = (VALUES[m][0] - COUNT // 2) * rows
+        end = first + len(VALUES[m]) * rows
+        low, high = first // DIM * DIM, -(-end // DIM) * DIM
+        entries = pl.ds(i * RANDOM, RANDOM)
+        values = [given[j][t, entries].reshape(rows, DIM) for j in VALUES[m]]
+        if first > low:
+            values = [jnp.zeros((first - low, DIM), jnp.bfloat16)] + values
+        if high > end:
+            values = values + [jnp.zeros((high - end, DIM), jnp.bfloat16)]
+        mixed = jnp.dot(
+            probs[n, :, low:high], jnp.concatenate(values, axis=0),
+            preferred_element_type=jnp.float32,
+        )
+        return i, h, mixed
 
     def middle(m):
         def step(n, carry):
@@ -371,86 +403,90 @@
         out_tile(i, h).start()
         return carry
 
-    def some(fn, low, high):
-        lax.fori_loop(low, high, fn, 0)
-
-    a, b = KEYS
-    ring_start(a)
-    ring_start(b)
-    keep_q.wait()
-    keep_k.wait()
-    keep_v.wait()
-    for side in sides:
-        side.wait_recv()
-    some(near, 0, 3)
-    ring_step(a, 1)
-    some(near, 3, 6)
-    for j in VALUES:
-        own_part(j).wait()
+    cost = {1: 4, 2: 4, 3: 3, 4: 1}
+    queue, begun, ahead_of = [], 0, 0
+    after = {}
+
+    def at(event, *parts):
+        after.setdefault(event, []).extend(parts)
+
+    def tasks(fn, low, high):
+        return lambda: lax.fori_loop(low, high, fn, 0)
+
+    def call(fn, *args):
+        return lambda: fn(*args)
+
+    def windows():
+        keep_q.wait()
+        keep_k.wait()
+        keep_v.wait()
+        for side in sides:
+            side.wait_recv()
+
+    def globals_ready():
+        for j in range(COUNT):
+            ring_ready(j)
+        split_globals()
+
+    def far_ready():
         for t in range(1, XS):
-            to_head(j, t).wait_recv()
-    split_globals()
-    ring_step(b, 1)
-    some(near, 6, 9)
-    ring_globals()
-    ring_step(a, 2)
-    some(near, 9, 12)
-    pass_globals(0)
-    pass_globals(4)
-    ring_step(b, 2)
-    some(near, 12, 14)
-    pass_globals(1)
-    pass_globals(5)
-    ring_step(a, 3)
-    some(near, 14, 16)
-    pass_globals(2)
-    pass_globals(6)
-    ring_step(b, 3)
-    pass_globals(3)
-    join_globals()
-    for j in VALUES:
-        hop(j, 0, 1).start()
-        hop(j, 1, 1).start()
-    ring_step(a, 4)
-    spread_globals()
-    ring_step(b, 4)
-    for j in VALUES:
-        choose(j, 0)
-    hand_out(a)
-    ring_step(VALUES[0], 1)
-    hand_out(b)
-    ring_step(VALUES[1], 1)
-    ring_step(VALUES[2], 1)
-    ring_step(VALUES[0], 2)
-    for t in range(1, XS):
-        widen(t).wait_recv()
-    take(a)
-    take(b)
-    ring_step(VALUES[1], 2)
-    some(far, 0, 2)
-    ring_step(VALUES[2], 2)
-    some(far, 2, 5)
-    ring_step(VALUES[0], 3)
-    some(far, 5, 8)
-    ring_step(VALUES[1], 3)
-    some(far, 8, 10)
-    ring_step(VALUES[2], 3)
-    some(far, 10, 12)
-    ring_step(VALUES[0], 4)
-    some(far, 12, 14)
-    hand_out(VALUES[0])
-    ring_step(VALUES[1], 4)
-    some(far, 14, 16)
-    hand_out(VALUES[1])
-    ring_step(VALUES[2], 4)
-    take(VALUES[0])
-    some(middle(0), 0, 8)
-    hand_out(VALUES[2])
-    some(middle(0), 8, 16)
-    take(VALUES[1])
-    some(middle(1), 0, 16)
-    take(VALUES[2])
-    some(last, 0, 16)
+            widen(t).wait_recv()
+        for j in KEYS:
+            take(j)
+
+    at(1, windows, tasks(near, 0, 2))
+    at(3, tasks(near, 2, 5))
+    at(5, tasks(near, 5, 8))
+    at(6, globals_ready)
+    at(8, tasks(near, 8, 12))
+    at(9, ring_globals)
+    at(11, tasks(near, 12, 16))
+    at(13, join_globals)
+    at(15, spread_globals)
+    FAR = 25
+    at(FAR, far_ready, tasks(far, 0, 2))
+    at(FAR + 2, tasks(far, 2, 5))
+    at(FAR + 4, tasks(far, 5, 8))
+    at(FAR + 5, tasks(far, 8, 9))
+
+    def begin():
+        nonlocal begun, ahead_of
+        while begun < COUNT and ahead_of < DEPTH:
+            ring_ready(begun)
+            ring_start(begun)
+            queue.append((begun, 1))
+            ahead_of += cost[1]
+            begun += 1
+
+    begin()
+    event = 0
+    handed = []
+    while queue:
+        j, step = queue.pop(0)
+        ring_step(j, step)
+        ahead_of -= cost[step]
+        if step < ZS // 2:
+            queue.append((j, step + 1))
+            ahead_of += cost[step + 1]
+        elif event + 2 < COUNT * ZS // 2 - 1:
+            at(event + 2, call(hand_out, j))
+            handed.append(j)
+        begin()
+        for part in after.pop(event, ()):
+            part()
+        event += 1
+    rest = [j for j in range(COUNT) if j not in handed]
+    lax.fori_loop(9, 11, far, 0)
+    for j in rest:
+        hand_out(j)
+    lax.fori_loop(11, TASKS, far, 0)
+    take(4)
+    take(5)
+    lax.fori_loop(0, TASKS, middle(0), 0)
+    take(6)
+    lax.fori_loop(0, TASKS, middle(1), 0)
+    take(7)
+    lax.fori_loop(0, TASKS, last, 0)
 
     for j in range(COUNT):
         for t in range(1, XS):
@@ -465,8 +501,8 @@
     whole = gfrom.at[1:PLANE]
     pltpu.make_async_copy(whole, whole, gbs).wait()
     pltpu.make_async_copy(whole, whole, gds).wait()
-    for n in range(ZS - 1):
-        hop_globals(n).wait_send()
+    for n in range(1, ZS):
+        to_plane(n).wait_send()
     for t in range(1, XS):
         widen(t).wait_send()
     pltpu.make_async_copy(qbuf, out_hbm, outs).wait()
@@ -481,39 +517,41 @@
     y, c = yc // CS, yc % CS
 
     refs = lax.dynamic_index_in_dim(random_table, x, 1, keepdims=False)
-    refs = refs.reshape(seq_count, RUN * RANDOM)
-    plane = lax.dynamic_slice_in_dim(refs, z * PLANE, PLANE, 0)
-    up = jnp.arange(ZS, dtype=jnp.int32)
-    senders = ((z - up) % ZS) * PLANE + yc
-    wanted = jnp.max(
-        jnp.where(plane[None] // RUN == senders[:, None, None], plane[None] % RUN, 0), axis=2
+    refs = refs.reshape(ZS, PLANE, RUN * RANDOM)
+    near_by = lax.dynamic_slice_in_dim(
+        jnp.concatenate([refs, refs], axis=0), (z + ZS - REACH) % ZS, SPAN, 0
     )
-    spots = jnp.array([SPOT[d] for d in range(ZS)], jnp.int32)
+    origins = ((z + jnp.arange(-REACH, REACH + 1, dtype=jnp.int32)) % ZS) * PLANE + yc
+    named_runs = near_by[:, None] // RUN == origins[None, :, None, None]
+    wanted = jnp.max(jnp.where(named_runs, near_by[:, None] % RUN, 0), axis=3)
 
     def across(owner):
         other = owner % PLANE
         return ((y - other // CS) % YS) * CS + (c - other % CS) % CS
 
-    mine = lax.dynamic_index_in_dim(plane, yc, 0, keepdims=False) // RUN
+    mine = lax.dynamic_index_in_dim(near_by[REACH], yc, 0, keepdims=False) // RUN
     up_of = lambda owner: (z - owner // PLANE) % ZS
-    lies = across(mine) * ZS + jnp.sum(
-        jnp.where(up_of(mine)[:, None] == up[None], spots[None], 0), axis=1
-    )
+    spot = jnp.zeros_like(mine)
+    for d in range(ZS):
+        spot = jnp.where(up_of(mine) == d, SPOT[d], spot)
+    lies = across(mine) * ZS + spot
     owners = global_blocks // RUN
-    table = jnp.concatenate(
-        [wanted.reshape(-1), lies, global_blocks % RUN, across(owners), up_of(owners)]
-    )
+    shared_at = jnp.concatenate([global_blocks % RUN, across(owners), up_of(owners)])
 
     vmem = lambda *shape: pltpu.VMEM(shape, jnp.bfloat16)
     dma = pltpu.SemaphoreType.DMA
-    sizes = [size for _, _, size in CHUNKS]
+    every = lambda *shape: [vmem(*shape) for _ in range(COUNT)]
+    passed = [d for d in range(ZS) if d <= REACH or d >= ZS - REACH]
     scratch = [
-        [[vmem(RUN, r, DIM) for _ in range(ZS)] for r in sizes],
-        [vmem(PLANE - 1, ZS, r, DIM) for r in sizes],
-        [vmem(PLANE * ZS, r, DIM) for r in sizes],
-        [vmem(XS - 1, NAMED, r, DIM) for r in sizes],
-        [vmem(XS, NAMED, r, DIM) for r in sizes],
-        [vmem(TASKS, LINES, RANDOM * sizes[v]) for v in VALUES],
+        [{d: vmem(RUN, SIZE, DIM) for d in passed} for _ in range(COUNT)],
+        every(2, SLOTS, SIZE, DIM),
+        every(2, SLOTS, SIZE, DIM),
+        every(PLANE, SIZE, DIM),
+        every(PLANE - 1, ZS, SIZE, DIM),
+        every(PLANE * ZS, SIZE, DIM),
+        every(XS - 1, NAMED, SIZE, DIM),
+        every(XS, NAMED, SIZE, DIM),
+        vmem(TASKS, LINES, RANDOM * BLOCK),
         vmem(rows, width),
         vmem(HERE + 2, BLOCK, XS * DIM),
         vmem(HERE + 2, BLOCK, XS * DIM),
@@ -537,14 +575,14 @@
     return pl.pallas_call(
         body,
         out_shape=jax.ShapeDtypeStruct((rows, width), jnp.bfloat16),
-        in_specs=[pl.BlockSpec(memory_space=pltpu.SMEM)] + [anywhere] * 3,
+        in_specs=[pl.BlockSpec(memory_space=pltpu.SMEM)] * 3 + [anywhere] * 3,
         out_specs=anywhere,
         scratch_shapes=scratch,
         compiler_params=pltpu.CompilerParams(
             collective_id=0, has_side_effects=True, vmem_limit_bytes=67_043_328
         ),
         name="attend",
-    )(table, query_rows, blocks(key_rows), blocks(value_rows))
+    )(wanted.reshape(-1), lies, shared_at, query_rows, blocks(key_rows), blocks(value_rows))
 
 
 def solution(mesh):

time: 152 us -> 137 us (0.901)
  Pallas kernels: 143 us -> 128 us
    pallas_call x1, Pallas kernels: 143 us -> 128 us  [on_device(): pl.pallas_call(body, out_shape=jax.ShapeDtypeStruct((rows, width), jnp.bf...]
where the time goes in v3:
time: 137 us
  Pallas kernels  128 us (93%)
  local copies, waits for them, and re-layouts  6.64 us (5%)
  other arithmetic  2.53 us (2%)
    pallas_call x1, Pallas kernels, on_device(): pl.pallas_call(body, out_shape=jax.ShapeDtypeStruct((rows, width), jnp.bf...  128 us
    unnamed x1, local copies, waits for them, and re-layouts  4.7 us

profile of v3, /device:TPU:1, one launch (start us, length us, event | category | flops | bytes accessed | tf_op | source)
XLA Modules:
  0.0 137.3 jit_solution(13500139252868623600)
XLA Ops:
  0.0 0.7 fusion.4
  0.7 0.6 pad_add_fusion.shared_at
  1.3 0.8 constant_dynamic-slice_fusion.1
  2.2 0.2 copy.7
  2.4 0.3 reshape.59
  2.7 0.6 fusion.10.lies
  3.3 0.6 select_reduce_fusion
  3.9 0.7 reshape.60.wanted
  4.5 128.1 %attend.1 = bf16[512,4096]{1,0:T(8,128)(2,1)} custom-call(s32[200]{0:T(256)} %reshape.60.wanted, s32[48]{0:T(128)} %fusion.10.lies, s32[6]{0:T(128)} %pad_add_fusion.shared_at, bf16[512,4096]{1,0:T(8,128)(2,1)} %q_hbm.1, bf16[4,128,512]{2,1,0:T(8,128)(2,1)} %bitcast.10, bf16[4,128,512]{2,1,0:T(8,128)(2,1)} %bitcast.11), custom_call_target="tpu_custom_call" | custom-call | tf_op jit(solution)/shard_map/attend/pallas_call | solution.py:575
  132.6 4.7 %copy.9 = bf16[512,4096]{1,0:T(8,128)(2,1)} copy(bf16[512,4096]{1,0:T(8,128)(2,1)} %attend.1) | data formatting | bytes 8388608
  (5 shorter events, 0.1 us)
